TPU v7x, 64 devices: a 2x2x8 block of a 4x4x8 slice. The times are simulated.
64 devices in a mesh: rep: 4 (over x, y), dp: 16 (over z, core).
Axes of the slice: x: 2, y: 2, z: 8, core: 2. Of those that a mesh axis runs over, the one named last changes fastest.
The devices are a block of a 4x4x8 slice.
Arguments:
- hidden: bfloat16 [2048, 5120], P(('rep', 'dp')), parts along dimension 0
- ckv_cache: bfloat16 [2048, 256, 512], P(('rep', 'dp')), parts along dimension 0
- kpe_cache: bfloat16 [2048, 256, 64], P(('rep', 'dp')), parts along dimension 0
- cache_len: int32 [2048], P(('rep', 'dp')), parts along dimension 0
- rope_cos: float32 [2048, 32], P(('rep', 'dp')), parts along dimension 0
- rope_sin: float32 [2048, 32], P(('rep', 'dp')), parts along dimension 0
- norm_attn: float32 [5120], replicated
- w_dq: bfloat16 [5120, 1536], replicated
- norm_q: float32 [1536], replicated
- w_uq: bfloat16 [1536, 128, 192], replicated
- w_dkv: bfloat16 [5120, 576], replicated
- norm_kv: float32 [512], replicated
- w_uk: bfloat16 [512, 128, 128], replicated
- w_uv: bfloat16 [512, 128, 128], replicated
- w_out: bfloat16 [128, 128, 5120], replicated
- norm_mlp: float32 [5120], replicated
- w_gate: bfloat16 [5120, 12288], P(None, 'dp')
- w_up: bfloat16 [5120, 12288], P(None, 'dp')
- w_down: bfloat16 [12288, 5120], P('dp')
Outputs:
- output 1: bfloat16 [2048, 5120], P(('rep', 'dp')), parts along dimension 0
- output 2: bfloat16 [2048, 512], P(('rep', 'dp')), parts along dimension 0
- output 3: bfloat16 [2048, 64], P(('rep', 'dp')), parts along dimension 0
There are 4 independent parts. A program takes and returns all parts, laid end to end along the dimension named above; an argument that names none is the same for every part.
All inputs are finite; a program needn't handle non-finite values.
Results may differ from a plain program's by a relative error of at most 0.0108911.
Values are sent between devices in bfloat16 or wider.
A program may use at most 768 MiB of HBM per device.

v0:
```python
import math
import jax
import jax.numpy as jnp
from jax import lax
from jax.sharding import PartitionSpec as P

EPSILON = 1e-6
MSCALE = 0.1 * math.log(40.0) + 1.0


def rms_norm(values_in, gain_vec):
    floats = values_in.astype(jnp.float32)
    mean_sq = jnp.mean(floats * floats, axis=-1, keepdims=True)
    return floats * lax.rsqrt(mean_sq + EPSILON) * gain_vec


def apply_rope(values_in, cos_t, sin_t):
    half_dim = values_in.shape[-1] // 2
    low_half = values_in[..., :half_dim]
    high_half = values_in[..., half_dim:]
    return jnp.concatenate([low_half * cos_t - high_half * sin_t, high_half * cos_t + low_half * sin_t], axis=-1)


def attention_rows(hidden, ckv_cache, kpe_cache, cache_len, rope_cos, rope_sin, norm_attn, w_dq, norm_q, w_uq, w_dkv, norm_kv, w_uk, w_uv, w_out):
    nope_dim = w_uk.shape[2]
    value_a7 = w_uk.shape[0]
    score_scale = MSCALE * MSCALE / math.sqrt(w_uq.shape[2])
    normed = rms_norm(hidden, norm_attn).astype(jnp.bfloat16)
    q_latent = rms_norm(jnp.dot(normed, w_dq, preferred_element_type=jnp.float32), norm_q).astype(jnp.bfloat16)
    q_full = jnp.einsum('bl,lhe->bhe', q_latent, w_uq, preferred_element_type=jnp.float32)
    q_nope = q_full[..., :nope_dim].astype(jnp.bfloat16)
    q_pe = apply_rope(q_full[..., nope_dim:], rope_cos[:, None, :], rope_sin[:, None, :]).astype(jnp.bfloat16)
    kv_full = jnp.dot(normed, w_dkv, preferred_element_type=jnp.float32)
    ckv_new = rms_norm(kv_full[:, :value_a7], norm_kv).astype(jnp.bfloat16)
    kpe_new = apply_rope(kv_full[:, value_a7:], rope_cos, rope_sin).astype(jnp.bfloat16)
    q_abs = jnp.einsum('bhn,lhn->bhl', q_nope, w_uk, preferred_element_type=jnp.float32).astype(jnp.bfloat16)
    scores = (jnp.einsum('bhl,btl->bht', q_abs, ckv_cache, preferred_element_type=jnp.float32)
              + jnp.einsum('bhr,btr->bht', q_pe, kpe_cache, preferred_element_type=jnp.float32)) * score_scale
    positions = jnp.arange(ckv_cache.shape[1])
    scores = jnp.where(positions[None, None, :] < cache_len[:, None, None], scores, -jnp.inf)
    score_new = (jnp.einsum('bhl,bl->bh', q_abs, ckv_new, preferred_element_type=jnp.float32)
                 + jnp.einsum('bhr,br->bh', q_pe, kpe_new, preferred_element_type=jnp.float32)) * score_scale
    row_max = jnp.maximum(jnp.max(scores, axis=-1), score_new)
    exp_cache = jnp.exp(scores - row_max[..., None])
    exp_new = jnp.exp(score_new - row_max)
    norm_sum = jnp.sum(exp_cache, axis=-1) + exp_new
    weighted = (jnp.einsum('bht,btl->bhl', exp_cache.astype(jnp.bfloat16), ckv_cache, preferred_element_type=jnp.float32)
                + exp_new.astype(jnp.bfloat16).astype(jnp.float32)[..., None] * ckv_new.astype(jnp.float32)[:, None, :])
    lat_out = (weighted / norm_sum[..., None]).astype(jnp.bfloat16)
    head_out = jnp.einsum('bhl,lhv->bhv', lat_out, w_uv, preferred_element_type=jnp.float32).astype(jnp.bfloat16)
    attn_out = jnp.einsum('bhv,hvd->bd', head_out, w_out, preferred_element_type=jnp.float32)
    residual = (hidden.astype(jnp.float32) + attn_out).astype(jnp.bfloat16)
    return residual, ckv_new, kpe_new


def solution(mesh):
    row_spec = P(('rep', 'dp'), None)
    cube_spec = P(('rep', 'dp'), None, None)
    full_spec = P()
    in_specs = (row_spec, cube_spec, cube_spec, P(('rep', 'dp')), row_spec, row_spec,
                full_spec, full_spec, full_spec, full_spec, full_spec, full_spec, full_spec, full_spec, full_spec, full_spec,
                P(None, 'dp'), P(None, 'dp'), P('dp', None))

    def local_step(hidden, ckv_cache, kpe_cache, cache_len, rope_cos, rope_sin, norm_attn, w_dq, norm_q, w_uq, w_dkv, norm_kv, w_uk, w_uv, w_out, norm_mlp, w_gate, w_up, w_down):
        residual, ckv_new, kpe_new = attention_rows(hidden, ckv_cache, kpe_cache, cache_len, rope_cos, rope_sin, norm_attn, w_dq, norm_q, w_uq, w_dkv, norm_kv, w_uk, w_uv, w_out)
        mlp_in = rms_norm(residual, norm_mlp).astype(jnp.bfloat16)
        group_in = lax.all_gather(mlp_in, 'dp', axis=0, tiled=True)
        gate_val = jnp.dot(group_in, w_gate, preferred_element_type=jnp.float32)
        up_val = jnp.dot(group_in, w_up, preferred_element_type=jnp.float32)
        act_val = (jax.nn.silu(gate_val) * up_val).astype(jnp.bfloat16)
        partial_sum = jnp.dot(act_val, w_down, preferred_element_type=jnp.float32)
        mlp_rows = lax.psum_scatter(partial_sum, 'dp', scatter_dimension=0, tiled=True)
        out_hidden = (residual.astype(jnp.float32) + mlp_rows).astype(jnp.bfloat16)
        return out_hidden, ckv_new, kpe_new

    return jax.shard_map(local_step, mesh=mesh, in_specs=in_specs, out_specs=(row_spec, row_spec, row_spec), check_vma=False)
```

profile of v0, /device:TPU:21, one launch (start us, length us, event | category | flops | bytes accessed | tf_op | source)
XLA Modules:
  0.0 414.7 jit_solution(613640447266036820)
XLA Ops:
  7.3 1.3 fusion.34
  8.6 1.4 copy.26
  10.0 1.4 copy.27
  11.4 4.6 %fusion.44 = f32[32,576]{1,0:T(8,128)S(1)} fusion(bf16[5120,576]{0,1:T(8,128)(2,1)} %param.29, bf16[32,5120]{1,0:T(8,128)(2,1)} %param.19, f32[5120]{0:T(1024)} %param.25, f32[32]{0:T(128)S(1)} %add_rsqrt_fusion.3), kind=kOutput, calls=%fused_computation.45 | convolution fusion | flops 189399040 | bytes 6320256 | tf_op jit(solution)/shard_map/dot_general | solution.py:33
  16.0 0.1 multiply_reduce_fusion.2
  16.1 0.7 subtract_convert_fusion.1
  16.8 0.7 iota_compare_fusion
  17.5 0.5 add_rsqrt_fusion.1
  18.0 8.5 %multiply_reduce_fusion.1 = (f32[32]{0:T(128)S(1)}, f32[32,1536]{1,0:T(8,128)S(1)}) fusion(bf16[5120,1536]{1,0:T(8,128)(2,1)} %param.26, bf16[32,5120]{1,0:T(8,128)(2,1)S(1)} %copy-done.2, f32[5120]{0:T(1024)S(1)} %copy-done.3, f32[32]{0:T(128)S(1)} %add_rsqrt_fusion.3), kind=kOutput, calls=%fused_computation.41 | convolution fusion | flops 504070112 | bytes 16273664 | tf_op jit(solution)/shard_map/dot_general | solution.py:29
  26.5 69.7 %fusion = f32[32,128,192]{1,0,2:T(8,128)} fusion(bf16[1536,128,192]{1,2,0:T(8,128)(2,1)} %param.28, f32[32,1536]{1,0:T(8,128)S(1)} %get-tuple-element.12, f32[1536]{0:T(1024)S(1)} %copy-done.15, f32[32]{0:T(128)S(1)} %add_rsqrt_fusion.2), kind=kOutput, calls=%fused_computation | convolution fusion | flops 2416066560 | bytes 78846080 | tf_op jit(solution)/shard_map/bl,lhe->bhe/dot_general | solution.py:30
  96.2 1.8 slice.48
  98.0 1.5 copy.23
  99.6 0.8 fusion.52
  100.3 50.9 %convert_bitcast_fusion = bf16[32,128,512]{2,0,1:T(8,128)(2,1)S(1)} fusion(bf16[32,128,128]{2,0,1:T(8,128)(2,1)S(1)} %copy.23, bf16[512,128,128]{2,1,0:T(8,128)(2,1)} %param.31), kind=kOutput, calls=%fused_computation.14 | convolution fusion | flops 538968064 | bytes 22020096 | tf_op jit(solution)/shard_map/bhn,lhn->bhl/dot_general | solution.py:36
  151.3 2.3 fusion.12
  153.6 6.6 %fusion.14 = f32[32,128,256]{2,1,0:T(8,128)S(1)} fusion(bf16[32,256,512]{2,1,0:T(8,128)(2,1)} %param.20, bf16[32,128,512]{2,0,1:T(8,128)(2,1)S(1)} %convert_bitcast_fusion), kind=kOutput, calls=%fused_computation.19 | convolution fusion | flops 1073741824 | bytes 16777216 | tf_op jit(solution)/shard_map/bhl,btl->bht/dot_general | solution.py:37
  160.2 0.1 fusion.73
  160.3 1.7 subtract_convert_fusion
  162.0 0.3 fusion.37
  162.3 1.3 fusion.53
  163.6 1.3 fusion.10
  165.0 4.2 %divide_convert_fusion = bf16[32,128,512]{2,1,0:T(8,128)(2,1)} fusion(f32[32,128]{1,0:T(8,128)S(1)} %get-tuple-element.10, f32[32,512]{1,0:T(8,128)S(1)} %get-tuple-element.3, f32[32,128]{1,0:T(8,128)S(1)} %get-tuple-element.9, bf16[32,256,512]{2,1,0:T(8,128)(2,1)S(1)} %bitcast.45, f32[32,128,256]{2,1,0:T(8,128)S(1)} %get-tuple-element.14, ...), kind=kOutput, calls=%fused_computation.6 | convolution fusion | flops 1084227584 | bytes 16891904 | tf_op jit(solution)/shard_map/bht,btl->bhl/dot_general | solution.py:47
  169.3 43.7 %fusion.25.clone.1.clone.4 = bf16[32,128,128]{2,0,1:T(8,128)(2,1)S(1)} fusion(bf16[512,128,128]{2,1,0:T(8,128)(2,1)} %param.32, bf16[32,128,512]{2,1,0:T(8,128)(2,1)} %divide_convert_fusion), kind=kOutput, calls=%fused_computation.25.clone.clone.clone.clone.clone.1 | convolution fusion | flops 537395200 | bytes 22020096 | tf_op jit(solution)/shard_map/bhl,lhv->bhv/dot_general | solution.py:50
  213.0 53.1 %multiply_reduce_fusion = (f32[32]{0:T(128)S(1)}, f32[32,5120]{1,0:T(8,128)S(1)}) fusion(bf16[128,128,5120]{2,1,0:T(8,128)(2,1)} %param.33, bf16[32,5120]{1,0:T(8,128)(2,1)S(1)} %copy-done.2, bf16[32,128,128]{2,0,1:T(8,128)(2,1)S(1)} %fusion.25.clone.1.clone.4), kind=kOutput, calls=%fused_computation.33 | convolution fusion | flops 5369692160 | bytes 169803904 | tf_op jit(solution)/shard_map/bhv,hvd->bd/dot_general | solution.py:51
  266.1 0.9 multiply_convert_fusion.1
  267.1 45.3 %all-gather.2.cloned.1.call-done = bf16[512,5120]{1,0:T(8,128)(2,1)} async-done(((bf16[32,5120]{1,0:T(8,128)(2,1)}), bf16[512,5120]{1,0:T(8,128)(2,1)}) %all-gather.2.cloned.1.call-update) | async-done | bytes 5242896 | tf_op jit(solution)/shard_map/all_gather | solution.py:67
  312.4 8.7 %fusion.58 = f32[512,768]{1,0:T(8,128)S(1)} fusion(bf16[512,5120]{1,0:T(8,128)(2,1)} %all-gather.2.cloned.1.call-done, bf16[5120,768]{1,0:T(8,128)(2,1)} %param.35), kind=kOutput, calls=%fused_computation.66 | convolution fusion | flops 4026531840 | bytes 14680064 | tf_op jit(solution)/shard_map/dot_general | solution.py:68
  321.2 7.6 %multiply_convert_fusion = bf16[512,768]{1,0:T(8,128)(2,1)S(1)} fusion(f32[512,768]{1,0:T(8,128)S(1)} %fusion.58, bf16[512,5120]{1,0:T(8,128)(2,1)S(1)} %copy-done.14, bf16[5120,768]{1,0:T(8,128)(2,1)} %param.36), kind=kOutput, calls=%fused_computation.23 | convolution fusion | flops 4028891136 | bytes 15466496 | tf_op jit(solution)/shard_map/dot_general | solution.py:69
  328.7 10.0 %fusion.59 = f32[512,5120]{1,0:T(8,128)} fusion(bf16[512,768]{1,0:T(8,128)(2,1)S(1)} %multiply_convert_fusion, bf16[768,5120]{1,0:T(8,128)(2,1)} %param.37), kind=kOutput, calls=%fused_computation.67 | convolution fusion | flops 4026531840 | bytes 19136512 | tf_op jit(solution)/shard_map/dot_general | solution.py:71
  338.8 0.7 pad_maximum_fusion.1
  339.5 66.2 %reduce-scatter.2.cloned.1.call-done = f32[32,5120]{1,0:T(8,128)} async-done(((f32[512,5120]{1,0:T(8,128)}), f32[32,5120]{1,0:T(8,128)}) %reduce-scatter.2.cloned.1.call-update) | async-done | bytes 655376 | tf_op jit(solution)/shard_map/reduce_scatter | solution.py:72
  405.7 1.9 add_convert_fusion
  (47 shorter events, 0.4 us)
Async XLA Ops:
  7.2 155.1 %copy-start = (bf16[32,256,64]{1,2,0:T(8,128)(2,1)S(1)}, bf16[32,256,64]{1,2,0:T(8,128)(2,1)}, u32[]{:S(2)}) copy-start(bf16[32,256,64]{1,2,0:T(8,128)(2,1)} %param.21) | copy-start | bytes 3145732
  7.2 10.8 %copy-start.2 = (bf16[32,5120]{1,0:T(8,128)(2,1)S(1)}, bf16[32,5120]{1,0:T(8,128)(2,1)}, u32[]{:S(2)}) copy-start(bf16[32,5120]{1,0:T(8,128)(2,1)} %param.19) | copy-start | bytes 983044
  7.2 8.9 %copy-start.9 = (f32[32,32]{1,0:T(8,128)S(1)}, f32[32,32]{1,0:T(8,128)}, u32[]{:S(2)}) copy-start(f32[32,32]{1,0:T(8,128)} %param.23) | copy-start | bytes 12292
  7.2 8.9 %copy-start.8 = (f32[32,32]{1,0:T(8,128)S(1)}, f32[32,32]{1,0:T(8,128)}, u32[]{:S(2)}) copy-start(f32[32,32]{1,0:T(8,128)} %param.24) | copy-start | bytes 12292
  7.2 10.8 %copy-start.3 = (f32[5120]{0:T(1024)S(1)}, f32[5120]{0:T(1024)}, u32[]{:S(2)}) copy-start(f32[5120]{0:T(1024)} %param.25) | copy-start | bytes 61444
  7.2 9.6 %copy-start.13 = (s32[32]{0:T(128)S(1)}, s32[32]{0:T(128)}, u32[]{:S(2)}) copy-start(s32[32]{0:T(128)} %param.22) | copy-start | bytes 388
  7.3 305.1 %all-gather.2.cloned.1.call-start = ((), (), s32[]{:S(2)}) async-start(), calls=%async_computation.1 | async-start | bytes 5570560 | tf_op jit(solution)/shard_map/all_gather | solution.py:67
  18.0 8.5 %copy-start.15 = (f32[1536]{0:T(1024)S(1)}, f32[1536]{0:T(1024)}, u32[]{:S(2)}) copy-start(f32[1536]{0:T(1024)} %param.27) | copy-start | bytes 18436
  100.3 50.9 %copy-start.10 = (bf16[32,512]{1,0:T(8,128)(2,1)}, bf16[32,512]{1,0:T(8,128)(2,1)S(1)}, u32[]{:S(2)}) copy-start(bf16[32,512]{1,0:T(8,128)(2,1)S(1)} %get-tuple-element.4) | copy-start | bytes 98308
  153.6 6.6 %copy-start.4 = (bf16[32,32]{1,0:T(8,128)(2,1)S(1)}, bf16[32,32]{1,0:T(8,128)(2,1)}, u32[]{:S(2)}) copy-start(bf16[32,32]{1,0:T(8,128)(2,1)} %get-tuple-element.7) | copy-start | bytes 6148
  153.6 6.6 %copy-start.5 = (bf16[32,32]{1,0:T(8,128)(2,1)S(1)}, bf16[32,32]{1,0:T(8,128)(2,1)}, u32[]{:S(2)}) copy-start(bf16[32,32]{1,0:T(8,128)(2,1)} %get-tuple-element.8) | copy-start | bytes 6148
  153.6 6.7 %copy-start.6 = (f32[32,32]{0,1:T(8,128)S(1)}, f32[32,32]{0,1:T(8,128)}, u32[]{:S(2)}) copy-start(f32[32,32]{0,1:T(8,128)} %copy.26) | copy-start | bytes 12292
  153.6 6.7 %copy-start.7 = (f32[32,32]{0,1:T(8,128)S(1)}, f32[32,32]{0,1:T(8,128)}, u32[]{:S(2)}) copy-start(f32[32,32]{0,1:T(8,128)} %copy.27) | copy-start | bytes 12292
  153.6 8.7 %copy-start.11 = (pred[32,256]{1,0:T(8,128)(4,1)S(1)}, pred[32,256]{1,0:T(8,128)(4,1)}, u32[]{:S(2)}) copy-start(pred[32,256]{1,0:T(8,128)(4,1)} %iota_compare_fusion) | copy-start | bytes 24580
  160.3 4.7 %slice-start = ((s8[8388608]{0:T(1024)(128)(4,1)}), s8[4194304]{0:T(1024)(128)(4,1)S(1)}, s32[]{:S(2)}) async-start(s8[8388608]{0:T(1024)(128)(4,1)} %bitcast.44), calls=%async_computation.3 | async-start | bytes 8388608
  162.3 2.7 slice-start.1
  213.0 53.1 %copy-start.12 = (f32[5120]{0:T(1024)S(1)}, f32[5120]{0:T(1024)}, u32[]{:S(2)}) copy-start(f32[5120]{0:T(1024)} %param.34) | copy-start | bytes 61444
  267.0 138.8 %reduce-scatter.2.cloned.1.call-start = ((), (), s32[]{:S(2)}) async-start(), calls=%async_computation.2 | async-start | bytes 11141120 | tf_op jit(solution)/shard_map/reduce_scatter | solution.py:72
  312.4 8.8 %copy-start.14 = (bf16[512,5120]{1,0:T(8,128)(2,1)S(1)}, bf16[512,5120]{1,0:T(8,128)(2,1)}, u32[]{:S(2)}) copy-start(bf16[512,5120]{1,0:T(8,128)(2,1)} %all-gather.2.cloned.1.call-done) | copy-start | bytes 15728644
  338.8 68.9 %copy-start.1 = (bf16[32,256,64]{1,2,0:T(8,128)(2,1)S(1)}, bf16[32,256,64]{1,2,0:T(8,128)(2,1)}, u32[]{:S(2)}) copy-start(bf16[32,256,64]{1,2,0:T(8,128)(2,1)} %param.21) | copy-start | bytes 3145732
Sparse Core Ops, SparseCore 0:
  267.1 45.2 all-gather.1
  338.9 66.7 reduce-scatter.1
where the time goes:
time: 420 us; the launch traced here: 415 us
  matrix products  271 us (65%)
  waiting for transfers between devices  112 us (27%)
  between operations  14.5 us (3%)
  other arithmetic  10.6 us (3%)
  local copies, waits for them, and re-layouts  6.24 us (1%)
    dot_general x1, matrix products, attention_rows(): jnp.einsum('bl,lhe->bhe', q_latent, w_uq, preferred_element_type=jnp.floa...  69.7 us
    reduce_scatter x1, waiting for transfers between devices, local_step(): lax.psum_scatter(partial_sum, 'dp', scatter_dimension=0, tiled=True)  66.2 us
    dot_general x1, matrix products, attention_rows(): jnp.einsum('bhv,hvd->bd', head_out, w_out, preferred_element_type=jnp.flo...  53.1 us
    dot_general x1, matrix products, attention_rows(): jnp.einsum('bhn,lhn->bhl', q_nope, w_uk, preferred_element_type=jnp.float32)  50.9 us
    all_gather x1, waiting for transfers between devices, local_step(): group_in = lax.all_gather(mlp_in, 'dp', axis=0, tiled=True)  45.3 us
    dot_general x1, matrix products, attention_rows(): jnp.einsum('bhl,lhv->bhv', lat_out, w_uv, preferred_element_type=jnp.floa...  43.7 us
    dot_general x1, matrix products, local_step(): partial_sum = jnp.dot(act_val, w_down, preferred_element_type=jnp.float32)  10 us
    dot_general x1, matrix products, local_step(): gate_val = jnp.dot(group_in, w_gate, preferred_element_type=jnp.float32)  8.74 us
  transfers between devices with their start and end apart: 2, of which 2 were waited for; matrix products, arithmetic and copies ran while one was open for 0% of the time, Pallas kernels for 0%

commit v1 on v0

--- a/solution.py
+++ b/solution.py
@@ -2,6 +2,8 @@
 import jax
 import jax.numpy as jnp
 from jax import lax
+from jax.experimental import pallas as pl
+from jax.experimental.pallas import tpu as pltpu
 from jax.sharding import PartitionSpec as P
 
 EPSILON = 1e-6
@@ -21,19 +23,210 @@
     return jnp.concatenate([low_half * cos_t - high_half * sin_t, high_half * cos_t + low_half * sin_t], axis=-1)
 
 
+GROUP = 8
+Q_DEPTH = 4096
+Q_PACK = 2
+HEAD_PACK = 4
+LANES = 128
+VMEM_BYTES = 60 * 1024 * 1024
+
+
+def lane_ids(shape, axis):
+    return lax.broadcasted_iota(jnp.int32, shape, axis)
+
+
+def q_kernel(cq_ref, cos_ref, sin_ref, wa_ref, wb_ref, oa_ref, ob_ref, spread):
+    step = pl.program_id(0)
+    rows, depth = cq_ref.shape
+    wide = LANES * GROUP
+
+    @pl.when(step == 0)
+    def _():
+        expand = (lane_ids((LANES, wide), 1) // GROUP == lane_ids((LANES, wide), 0)).astype(jnp.bfloat16)
+        mine = lane_ids((rows, wide), 1) % GROUP == lane_ids((rows, wide), 0) % GROUP
+        for k in range(depth // LANES):
+            part = jnp.dot(cq_ref[:, k * LANES:(k + 1) * LANES], expand, preferred_element_type=jnp.float32)
+            spread[:, k * wide:(k + 1) * wide] = jnp.where(mine, part, 0.0).astype(jnp.bfloat16)
+
+    plain = step < pl.num_programs(0) * 2 // 3
+    for part in range(Q_PACK):
+        acc = jnp.zeros((rows, 2 * LANES), jnp.float32)
+        count = Q_DEPTH // GROUP
+        for at in range(0, depth, count):
+            both = jnp.concatenate([wa_ref[at:at + count, part * GROUP:(part + 1) * GROUP, :].reshape(Q_DEPTH, LANES),
+                                    wb_ref[at:at + count, part * GROUP:(part + 1) * GROUP, :].reshape(Q_DEPTH, LANES)], axis=1)
+            acc = acc + jnp.dot(spread[:, at * GROUP:at * GROUP + Q_DEPTH], both, preferred_element_type=jnp.float32)
+        low = acc[:, :LANES]
+        high = acc[:, LANES:]
+        cos_c = cos_ref[part]
+        sin_c = sin_ref[part]
+        first = jnp.where(plain, low, low * cos_c - high * sin_c)
+        second = jnp.where(plain, high, high * cos_c + low * sin_c)
+        batch = rows // GROUP
+        oa_ref[:, part * GROUP:(part + 1) * GROUP, :] = first.reshape(batch, GROUP, LANES).astype(jnp.bfloat16)
+        ob_ref[:, part * GROUP:(part + 1) * GROUP, :] = second.reshape(batch, GROUP, LANES).astype(jnp.bfloat16)
+
+
+def q_project(q_latent, w_uq, rope_cos, rope_sin):
+    batch, depth = q_latent.shape
+    heads, width = w_uq.shape[1], w_uq.shape[2]
+    stored = jnp.transpose(w_uq, (0, 2, 1))
+    rows = batch * GROUP
+    repeated = jnp.broadcast_to(q_latent[:, None, :], (batch, GROUP, depth)).reshape(rows, depth)
+    half = rope_cos.shape[1]
+    turns = half // (GROUP * Q_PACK)
+    nope = (width - 2 * half) // (2 * GROUP * Q_PACK)
+    cos_c = rope_cos.reshape(batch, half // GROUP, GROUP).transpose(1, 0, 2).reshape(half // GROUP, rows, 1)
+    sin_c = rope_sin.reshape(batch, half // GROUP, GROUP).transpose(1, 0, 2).reshape(half // GROUP, rows, 1)
+    steps = nope + turns
+
+    def first_at(j):
+        return (0, jnp.where(j < nope, j, j + nope), 0)
+
+    def second_at(j):
+        return (0, jnp.where(j < nope, j + nope, j + nope + turns), 0)
+
+    def turn_at(j):
+        return (jnp.maximum(j - nope, 0), 0, 0)
+
+    out_a, out_b = pl.pallas_call(
+        q_kernel,
+        grid=(steps,),
+        in_specs=[pl.BlockSpec((rows, depth), lambda j: (0, 0)),
+                  pl.BlockSpec((Q_PACK, rows, 1), turn_at), pl.BlockSpec((Q_PACK, rows, 1), turn_at),
+                  pl.BlockSpec((depth, Q_PACK * GROUP, heads), first_at), pl.BlockSpec((depth, Q_PACK * GROUP, heads), second_at)],
+        out_specs=[pl.BlockSpec((batch, Q_PACK * GROUP, heads), lambda j: (0, j, 0))] * 2,
+        out_shape=[jax.ShapeDtypeStruct((batch, steps * Q_PACK * GROUP, heads), jnp.bfloat16)] * 2,
+        scratch_shapes=[pltpu.VMEM((rows, depth * GROUP), jnp.bfloat16)],
+        compiler_params=pltpu.CompilerParams(vmem_limit_bytes=VMEM_BYTES),
+        cost_estimate=pl.CostEstimate(flops=2 * batch * depth * heads * width, bytes_accessed=2 * depth * heads * width, transcendentals=0),
+        name='q_project',
+    )(repeated, cos_c, sin_c, stored, stored)
+    cut = nope * Q_PACK * GROUP
+    q_nope = jnp.concatenate([out_a[:, :cut], out_b[:, :cut]], axis=1).transpose(0, 2, 1)
+    q_pe = jnp.concatenate([out_a[:, cut:], out_b[:, cut:]], axis=1).transpose(0, 2, 1)
+    return q_nope, q_pe
+
+
+def absorb_kernel(q_ref, w_ref, o_ref, plain):
+    batch, heads, inner = q_ref.shape
+    outer = w_ref.shape[0]
+    rows = batch * GROUP
+    own = lane_ids((rows, inner), 0) % GROUP
+    for part in range(heads // GROUP):
+        span = slice(part * GROUP, (part + 1) * GROUP)
+        plain[part] = w_ref[:, span, :].reshape(outer * GROUP, inner).astype(jnp.float32)
+        queries = q_ref[:, span, :].reshape(rows, inner)
+        acc = jnp.zeros((rows, outer), jnp.float32)
+        for h in range(0, GROUP, 2):
+            left = jnp.concatenate([jnp.where(own == h, queries, jnp.zeros_like(queries)),
+                                    jnp.where(own == h + 1, queries, jnp.zeros_like(queries))], axis=1)
+            right = jnp.concatenate([plain[part, pl.ds(h, outer, stride=GROUP), :].astype(jnp.bfloat16),
+                                     plain[part, pl.ds(h + 1, outer, stride=GROUP), :].astype(jnp.bfloat16)], axis=1)
+            acc = acc + lax.dot_general(left, right, (((1,), (1,)), ((), ())), preferred_element_type=jnp.float32)
+        o_ref[:, span, :] = acc.reshape(batch, GROUP, outer).astype(jnp.bfloat16)
+
+
+def absorb(q_nope, w_uk):
+    batch, heads, inner = q_nope.shape
+    outer = w_uk.shape[0]
+    return pl.pallas_call(
+        absorb_kernel,
+        grid=(heads // (HEAD_PACK * GROUP),),
+        in_specs=[pl.BlockSpec((batch, HEAD_PACK * GROUP, inner), lambda g: (0, g, 0)),
+                  pl.BlockSpec((outer, HEAD_PACK * GROUP, inner), lambda g: (0, g, 0))],
+        out_specs=pl.BlockSpec((batch, HEAD_PACK * GROUP, outer), lambda g: (0, g, 0)),
+        out_shape=jax.ShapeDtypeStruct((batch, heads, outer), jnp.bfloat16),
+        scratch_shapes=[pltpu.VMEM((HEAD_PACK, outer * GROUP, inner), jnp.float32)],
+        compiler_params=pltpu.CompilerParams(vmem_limit_bytes=VMEM_BYTES),
+        cost_estimate=pl.CostEstimate(flops=2 * batch * heads * inner * outer, bytes_accessed=2 * heads * inner * outer, transcendentals=0),
+        name='absorb',
+    )(q_nope, w_uk)
+
+
+def value_kernel(l_ref, w_ref, o_ref, plain, picked):
+    batch, heads, outer = l_ref.shape
+    inner = w_ref.shape[2]
+    rows = batch * GROUP
+    own = lane_ids((rows, inner), 0) % GROUP
+    for part in range(heads // GROUP):
+        span = slice(part * GROUP, (part + 1) * GROUP)
+        plain[part] = w_ref[:, span, :].reshape(outer * GROUP, inner).astype(jnp.float32)
+        latents = l_ref[:, span, :].reshape(rows, outer)
+        acc = jnp.zeros((rows, inner), jnp.float32)
+        for h in range(0, GROUP, 2):
+            right = jnp.concatenate([plain[part, pl.ds(h, outer, stride=GROUP), :].astype(jnp.bfloat16),
+                                     plain[part, pl.ds(h + 1, outer, stride=GROUP), :].astype(jnp.bfloat16)], axis=1)
+            both = jnp.dot(latents, right, preferred_element_type=jnp.float32)
+            acc = jnp.where(own == h, both[:, :inner], jnp.where(own == h + 1, both[:, inner:], acc))
+        picked[part] = acc
+        for h in range(GROUP):
+            o_ref[:, (part * GROUP + h) * inner:(part * GROUP + h + 1) * inner] = picked[part, pl.ds(h, batch, stride=GROUP), :].astype(jnp.bfloat16)
+
+
+def value_heads(lat_out, w_uv):
+    batch, heads, outer = lat_out.shape
+    inner = w_uv.shape[2]
+    return pl.pallas_call(
+        value_kernel,
+        grid=(heads // (HEAD_PACK * GROUP),),
+        in_specs=[pl.BlockSpec((batch, HEAD_PACK * GROUP, outer), lambda g: (0, g, 0)),
+                  pl.BlockSpec((outer, HEAD_PACK * GROUP, inner), lambda g: (0, g, 0))],
+        out_specs=pl.BlockSpec((batch, HEAD_PACK * GROUP * inner), lambda g: (0, g)),
+        out_shape=jax.ShapeDtypeStruct((batch, heads * inner), jnp.bfloat16),
+        scratch_shapes=[pltpu.VMEM((HEAD_PACK, outer * GROUP, inner), jnp.float32), pltpu.VMEM((HEAD_PACK, batch * GROUP, inner), jnp.float32)],
+        compiler_params=pltpu.CompilerParams(vmem_limit_bytes=VMEM_BYTES),
+        cost_estimate=pl.CostEstimate(flops=2 * batch * heads * inner * outer, bytes_accessed=2 * heads * inner * outer, transcendentals=0),
+        name='value_heads',
+    )(lat_out, w_uv)
+
+
+def out_kernel(o_ref, x_ref, w_ref, r_ref, acc):
+    step = pl.program_id(0)
+
+    @pl.when(step == 0)
+    def _():
+        acc[...] = x_ref[...].astype(jnp.float32)
+
+    acc[...] += jnp.dot(o_ref[...], w_ref[...], preferred_element_type=jnp.float32)
+
+    @pl.when(step == pl.num_programs(0) - 1)
+    def _():
+        r_ref[...] = acc[...].astype(jnp.bfloat16)
+
+
+OUT_PARTS = 4
+OUT_DEPTH = 4096
+
+
+def out_columns(head_out, hidden, w_flat, part):
+    batch, depth = head_out.shape
+    columns = w_flat.shape[1] // OUT_PARTS
+    return pl.pallas_call(
+        out_kernel,
+        grid=(depth // OUT_DEPTH,),
+        in_specs=[pl.BlockSpec((batch, OUT_DEPTH), lambda k: (0, k)),
+                  pl.BlockSpec((batch, columns), lambda k: (0, part)),
+                  pl.BlockSpec((OUT_DEPTH, columns), lambda k: (k, part))],
+        out_specs=pl.BlockSpec((batch, columns), lambda k: (0, 0)),
+        out_shape=jax.ShapeDtypeStruct((batch, columns), jnp.bfloat16),
+        scratch_shapes=[pltpu.VMEM((batch, columns), jnp.float32)],
+        compiler_params=pltpu.CompilerParams(vmem_limit_bytes=VMEM_BYTES),
+        cost_estimate=pl.CostEstimate(flops=2 * batch * depth * columns * 16, bytes_accessed=2 * depth * columns, transcendentals=0),
+        name='out_columns',
+    )(head_out, hidden, w_flat)
+
+
 def attention_rows(hidden, ckv_cache, kpe_cache, cache_len, rope_cos, rope_sin, norm_attn, w_dq, norm_q, w_uq, w_dkv, norm_kv, w_uk, w_uv, w_out):
-    nope_dim = w_uk.shape[2]
     value_a7 = w_uk.shape[0]
     score_scale = MSCALE * MSCALE / math.sqrt(w_uq.shape[2])
     normed = rms_norm(hidden, norm_attn).astype(jnp.bfloat16)
     q_latent = rms_norm(jnp.dot(normed, w_dq, preferred_element_type=jnp.float32), norm_q).astype(jnp.bfloat16)
-    q_full = jnp.einsum('bl,lhe->bhe', q_latent, w_uq, preferred_element_type=jnp.float32)
-    q_nope = q_full[..., :nope_dim].astype(jnp.bfloat16)
-    q_pe = apply_rope(q_full[..., nope_dim:], rope_cos[:, None, :], rope_sin[:, None, :]).astype(jnp.bfloat16)
+    q_nope, q_pe = q_project(q_latent, w_uq, rope_cos, rope_sin)
     kv_full = jnp.dot(normed, w_dkv, preferred_element_type=jnp.float32)
     ckv_new = rms_norm(kv_full[:, :value_a7], norm_kv).astype(jnp.bfloat16)
     kpe_new = apply_rope(kv_full[:, value_a7:], rope_cos, rope_sin).astype(jnp.bfloat16)
-    q_abs = jnp.einsum('bhn,lhn->bhl', q_nope, w_uk, preferred_element_type=jnp.float32).astype(jnp.bfloat16)
+    q_abs = absorb(q_nope, w_uk)
     scores = (jnp.einsum('bhl,btl->bht', q_abs, ckv_cache, preferred_element_type=jnp.float32)
               + jnp.einsum('bhr,btr->bht', q_pe, kpe_cache, preferred_element_type=jnp.float32)) * score_scale
     positions = jnp.arange(ckv_cache.shape[1])
@@ -47,10 +240,10 @@
     weighted = (jnp.einsum('bht,btl->bhl', exp_cache.astype(jnp.bfloat16), ckv_cache, preferred_element_type=jnp.float32)
                 + exp_new.astype(jnp.bfloat16).astype(jnp.float32)[..., None] * ckv_new.astype(jnp.float32)[:, None, :])
     lat_out = (weighted / norm_sum[..., None]).astype(jnp.bfloat16)
-    head_out = jnp.einsum('bhl,lhv->bhv', lat_out, w_uv, preferred_element_type=jnp.float32).astype(jnp.bfloat16)
-    attn_out = jnp.einsum('bhv,hvd->bd', head_out, w_out, preferred_element_type=jnp.float32)
-    residual = (hidden.astype(jnp.float32) + attn_out).astype(jnp.bfloat16)
-    return residual, ckv_new, kpe_new
+    head_out = value_heads(lat_out, w_uv)
+    w_flat = w_out.reshape(w_out.shape[0] * w_out.shape[1], w_out.shape[2])
+    parts = [out_columns(head_out, hidden, w_flat, part) for part in range(OUT_PARTS)]
+    return parts, ckv_new, kpe_new
 
 
 def solution(mesh):
@@ -62,9 +255,10 @@
                 P(None, 'dp'), P(None, 'dp'), P('dp', None))
 
     def local_step(hidden, ckv_cache, kpe_cache, cache_len, rope_cos, rope_sin, norm_attn, w_dq, norm_q, w_uq, w_dkv, norm_kv, w_uk, w_uv, w_out, norm_mlp, w_gate, w_up, w_down):
-        residual, ckv_new, kpe_new = attention_rows(hidden, ckv_cache, kpe_cache, cache_len, rope_cos, rope_sin, norm_attn, w_dq, norm_q, w_uq, w_dkv, norm_kv, w_uk, w_uv, w_out)
-        mlp_in = rms_norm(residual, norm_mlp).astype(jnp.bfloat16)
-        group_in = lax.all_gather(mlp_in, 'dp', axis=0, tiled=True)
+        parts, ckv_new, kpe_new = attention_rows(hidden, ckv_cache, kpe_cache, cache_len, rope_cos, rope_sin, norm_attn, w_dq, norm_q, w_uq, w_dkv, norm_kv, w_uk, w_uv, w_out)
+        gathered = [lax.all_gather(part, 'dp', axis=0, tiled=True) for part in parts]
+        residual = jnp.concatenate(parts, axis=1)
+        group_in = rms_norm(jnp.concatenate(gathered, axis=1), norm_mlp).astype(jnp.bfloat16)
         gate_val = jnp.dot(group_in, w_gate, preferred_element_type=jnp.float32)
         up_val = jnp.dot(group_in, w_up, preferred_element_type=jnp.float32)
         act_val = (jax.nn.silu(gate_val) * up_val).astype(jnp.bfloat16)

time: 420 us -> 391 us (0.931)
  matrix products: 271 us -> 59.9 us
  Pallas kernels: 0 us -> 125 us
  waiting for transfers between devices: 112 us -> 164 us
  local copies, waits for them, and re-layouts: 6.24 us -> 12.1 us
    dot_general x5 -> x0, matrix products: 226 us -> none  [the longest x1 69.7 us: attention_rows(): jnp.einsum('bl,lhe->bhe', q_latent, w_uq, preferred_element_type=jnp.floa...]
    pallas_call x0 -> x7, Pallas kernels: none -> 125 us  [the longest x4 66 us: out_columns(): pl.pallas_call(out_kernel, grid=(depth // OUT_DEPTH,), in_specs=[pl.Block...]
    all_gather x1 -> x4, waiting for transfers between devices: 45.3 us -> 97.6 us  [local_step(): lax.all_gather(part, 'dp', axis=0, tiled=True)]
    dot_general x1, matrix products: 10 us -> 19.7 us  [local_step(): partial_sum = jnp.dot(act_val, w_down, preferred_element_type=jnp.float32)]
  transfers between devices with their start and end apart: 2 -> 5, of which waited for: 2 -> 4; matrix products, arithmetic and copies ran while one was open for 0% -> 0% of each run, Pallas kernels for 0% -> 13%
where the time goes in v1:
time: 391 us; the launch traced here: 389 us
  waiting for transfers between devices  164 us (42%)
  Pallas kernels  125 us (32%)
  matrix products  59.9 us (15%)
  between operations  14.1 us (4%)
  other arithmetic  13.9 us (4%)
  local copies, waits for them, and re-layouts  12.1 us (3%)
    all_gather x4, waiting for transfers between devices, local_step(): lax.all_gather(part, 'dp', axis=0, tiled=True)  97.6 us
    pallas_call x4, Pallas kernels, out_columns(): pl.pallas_call(out_kernel, grid=(depth // OUT_DEPTH,), in_specs=[pl.Block...  66 us
    reduce_scatter x1, waiting for transfers between devices, local_step(): lax.psum_scatter(partial_sum, 'dp', scatter_dimension=0, tiled=True)  65.7 us
    pallas_call x1, Pallas kernels, q_project(): pl.pallas_call(q_kernel, grid=(steps,), in_specs=[pl.BlockSpec((rows, dep...  32 us
    dot_general x1, matrix products, local_step(): partial_sum = jnp.dot(act_val, w_down, preferred_element_type=jnp.float32)  19.7 us
    pallas_call x1, Pallas kernels, value_heads(): pl.pallas_call(value_kernel, grid=(heads // (HEAD_PACK * GROUP),), in_spe...  13.7 us
    pallas_call x1, Pallas kernels, absorb(): pl.pallas_call(absorb_kernel, grid=(heads // (HEAD_PACK * GROUP),), in_sp...  13.3 us
    dot_general x1, matrix products, local_step(): up_val = jnp.dot(group_in, w_up, preferred_element_type=jnp.float32)  8.69 us
  transfers between devices with their start and end apart: 5, of which 4 were waited for; matrix products, arithmetic and copies ran while one was open for 0% of the time, Pallas kernels for 13%

profile of v1, /device:TPU:21, one launch (start us, length us, event | category | flops | bytes accessed | tf_op | source)
XLA Modules:
  0.0 389.0 jit_solution(11675182086813127408)
XLA Ops:
  7.3 1.2 fusion.13
  10.1 4.6 %fusion.17 = f32[32,576]{1,0:T(8,128)S(1)} fusion(bf16[5120,576]{0,1:T(8,128)(2,1)} %param.29, bf16[32,5120]{1,0:T(8,128)(2,1)} %x_ref.7, f32[5120]{0:T(1024)} %param.25, f32[32]{0:T(128)S(1)} %add_rsqrt_fusion.3), kind=kOutput, calls=%fused_computation.27 | convolution fusion | flops 189399040 | bytes 6320256 | tf_op jit(solution)/shard_map/dot_general | solution.py:226
  15.8 8.4 %multiply_reduce_fusion = (f32[32]{0:T(128)S(1)}, f32[32,1536]{1,0:T(8,128)S(1)}) fusion(bf16[5120,1536]{1,0:T(8,128)(2,1)} %param.26, bf16[32,5120]{1,0:T(8,128)(2,1)S(1)} %copy-done.3, f32[5120]{0:T(1024)S(1)} %copy-done.12, f32[32]{0:T(128)S(1)} %add_rsqrt_fusion.3), kind=kOutput, calls=%fused_computation.26 | convolution fusion | flops 504070112 | bytes 16273664 | tf_op jit(solution)/shard_map/dot_general | solution.py:224
  24.2 1.0 reshape.96.cos_ref
  25.2 1.0 reshape.97.sin_ref
  26.3 1.0 broadcast_bitcast_fusion.cq_ref
  27.3 32.0 %q_project.1 = (bf16[32,96,128]{2,1,0:T(8,128)(2,1)}, bf16[32,96,128]{2,1,0:T(8,128)(2,1)}) custom-call(bf16[256,1536]{1,0:T(8,128)(2,1)} %broadcast_bitcast_fusion.cq_ref, f32[4,256,1]{2,1,0:T(8,128)} %reshape.96.cos_ref, f32[4,256,1]{2,1,0:T(8,128)} %reshape.97.sin_ref, bf16[1536,192,128]{2,1,0:T(8,128)(2,1)} %bitcast.5.wa_ref.wb_ref, ...), custom_call_target="tpu_custom_call" | custom-call | flops 2415919104 | bytes 75497472 | tf_op jit(solution)/shard_map/q_project/pallas_call | solution.py:92
  59.3 1.7 slice.27
  61.0 1.6 copy.33
  62.6 1.7 slice.26
  64.3 1.6 copy.32
  67.3 1.6 maximum_bitcast_fusion.q_ref
  68.9 13.3 %absorb.1 = bf16[32,128,512]{2,1,0:T(8,128)(2,1)} custom-call(bf16[32,128,128]{2,1,0:T(8,128)(2,1)} %maximum_bitcast_fusion.q_ref, bf16[512,128,128]{2,1,0:T(8,128)(2,1)} %w_ref.2), custom_call_target="tpu_custom_call" | custom-call | flops 536870912 | bytes 16777216 | tf_op jit(solution)/shard_map/absorb/pallas_call | solution.py:133
  82.2 4.1 %fusion.21 = f32[32,1,128]{2,1,0:T(1,128)} fusion(bf16[32,128,512]{2,1,0:T(8,128)(2,1)} %absorb.1, bf16[32,512,1]{1,0,2:T(8,128)(2,1)} %bitcast.35), kind=kOutput, calls=%fused_computation.29 | convolution fusion | flops 4194304 | bytes 4243456 | tf_op jit(solution)/shard_map/bhl,bl->bh/dot_general | solution.py:234
  86.3 6.4 %fusion.33 = f32[32,128,256]{2,1,0:T(8,128)S(1)} fusion(bf16[32,128,512]{2,1,0:T(8,128)(2,1)S(1)} %copy-done.2, bf16[32,256,512]{2,1,0:T(8,128)(2,1)} %param.20), kind=kOutput, calls=%fused_computation.52 | convolution fusion | flops 1073741824 | bytes 16777216 | tf_op jit(solution)/shard_map/bhl,btl->bht/dot_general | solution.py:230
  93.5 1.3 fusion.16
  94.7 2.4 fusion.32
  97.2 1.3 fusion.3
  98.6 4.3 %divide_convert_fusion.l_ref = bf16[32,128,512]{2,1,0:T(8,128)(2,1)} fusion(f32[32,128]{1,0:T(8,128)S(1)} %get-tuple-element.12, f32[32,512]{1,0:T(8,128)S(1)} %copy-done.19, f32[32,128]{1,0:T(8,128)S(1)} %get-tuple-element.11, bf16[32,256,512]{2,1,0:T(8,128)(2,1)S(1)} %bitcast.32, f32[32,128,256]{2,1,0:T(8,128)S(1)} %get-tuple-element.16, ...), kind=kOutput, calls=%fused_computation.5 | convolution fusion | flops 1084227584 | bytes 16891904 | tf_op jit(solution)/shard_map/bht,btl->bhl/dot_general | solution.py:240
  102.8 13.7 %value_heads.1.o_ref = bf16[32,16384]{1,0:T(8,128)(2,1)} custom-call(bf16[32,128,512]{2,1,0:T(8,128)(2,1)} %divide_convert_fusion.l_ref, bf16[512,128,128]{2,1,0:T(8,128)(2,1)} %w_ref.3), custom_call_target="tpu_custom_call" | custom-call | flops 536870912 | bytes 16777216 | tf_op jit(solution)/shard_map/value_heads/pallas_call | solution.py:170
  116.6 16.4 %out_columns.7 = bf16[32,1280]{1,0:T(8,128)(2,1)} custom-call(bf16[32,16384]{1,0:T(8,128)(2,1)} %value_heads.1.o_ref, bf16[32,5120]{1,0:T(8,128)(2,1)} %x_ref.7, bf16[16384,5120]{1,0:T(8,128)(2,1)} %bitcast.13.w_ref), custom_call_target="tpu_custom_call" | custom-call | flops 21474836480 | bytes 41943040 | tf_op jit(solution)/shard_map/out_columns/pallas_call | solution.py:205
  133.1 16.4 %out_columns.6 = bf16[32,1280]{1,0:T(8,128)(2,1)} custom-call(bf16[32,16384]{1,0:T(8,128)(2,1)} %value_heads.1.o_ref, bf16[32,5120]{1,0:T(8,128)(2,1)} %x_ref.7, bf16[16384,5120]{1,0:T(8,128)(2,1)} %bitcast.13.w_ref), custom_call_target="tpu_custom_call" | custom-call | flops 21474836480 | bytes 41943040 | tf_op jit(solution)/shard_map/out_columns/pallas_call | solution.py:205
  149.7 16.6 %out_columns.4 = bf16[32,1280]{1,0:T(8,128)(2,1)} custom-call(bf16[32,16384]{1,0:T(8,128)(2,1)} %value_heads.1.o_ref, bf16[32,5120]{1,0:T(8,128)(2,1)} %x_ref.7, bf16[16384,5120]{1,0:T(8,128)(2,1)} %bitcast.13.w_ref), custom_call_target="tpu_custom_call" | custom-call | flops 21474836480 | bytes 41943040 | tf_op jit(solution)/shard_map/out_columns/pallas_call | solution.py:205
  166.4 16.5 %out_columns.5 = bf16[32,1280]{1,0:T(8,128)(2,1)} custom-call(bf16[32,16384]{1,0:T(8,128)(2,1)} %value_heads.1.o_ref, bf16[32,5120]{1,0:T(8,128)(2,1)} %x_ref.7, bf16[16384,5120]{1,0:T(8,128)(2,1)} %bitcast.13.w_ref), custom_call_target="tpu_custom_call" | custom-call | flops 21474836480 | bytes 41943040 | tf_op jit(solution)/shard_map/out_columns/pallas_call | solution.py:205
  183.1 26.4 %all-gather.9.cloned.1.call-done = bf16[512,1280]{1,0:T(8,128)(2,1)} async-done(((bf16[32,1280]{1,0:T(8,128)(2,1)}), bf16[512,1280]{1,0:T(8,128)(2,1)}) %all-gather.9.cloned.1.call-update) | async-done | bytes 1310736 | tf_op jit(solution)/shard_map/all_gather | solution.py:259
  209.5 35.7 %all-gather.5.cloned.1.call-done = bf16[512,1280]{1,0:T(8,128)(2,1)} async-done(((bf16[32,1280]{1,0:T(8,128)(2,1)}), bf16[512,1280]{1,0:T(8,128)(2,1)}) %all-gather.5.cloned.1.call-update) | async-done | bytes 1310736 | tf_op jit(solution)/shard_map/all_gather | solution.py:259
  245.2 35.5 %all-gather.7.cloned.1.call-done = bf16[512,1280]{1,0:T(8,128)(2,1)} async-done(((bf16[32,1280]{1,0:T(8,128)(2,1)}), bf16[512,1280]{1,0:T(8,128)(2,1)}) %all-gather.7.cloned.1.call-update) | async-done | bytes 1310736 | tf_op jit(solution)/shard_map/all_gather | solution.py:259
  280.7 4.1 %fusion = f32[512]{0:T(512)S(1)} fusion(bf16[512,1280]{1,0:T(8,128)(2,1)} %all-gather.11.cloned.1.call-done, bf16[512,1280]{1,0:T(8,128)(2,1)} %all-gather.9.cloned.1.call-done, bf16[512,1280]{1,0:T(8,128)(2,1)} %all-gather.7.cloned.1.call-done, bf16[512,1280]{1,0:T(8,128)(2,1)} %all-gather.5.cloned.1.call-done), kind=kLoop, calls=%fused_computation.2 | loop fusion | flops 26213888 | bytes 5244928 | tf_op jit(solution)/shard_map/reduce_sum | solution.py:15
  284.9 8.7 %fusion.7 = f32[512,768]{1,0:T(8,128)} fusion(bf16[5120,768]{1,0:T(8,128)(2,1)} %param.36, f32[5120]{0:T(1024)S(1)} %copy-done.23, f32[512]{0:T(512)S(1)} %add_rsqrt_fusion, bf16[512,1280]{1,0:T(8,128)(2,1)S(1)} %copy-done.4, bf16[512,1280]{1,0:T(8,128)(2,1)S(1)} %copy-done.5, bf16[512,1280]{1,0:T(8,128)(2,1)S(1)} %copy-done.7, ...), kind=kOutput, calls=%fused_computation.13 | convolution fusion | flops 4055367680 | bytes 14702592 | tf_op jit(solution)/shard_map/dot_general | solution.py:263
  293.6 19.7 %fusion.29 = f32[512,5120]{1,0:T(8,128)} fusion(bf16[768,5120]{1,0:T(8,128)(2,1)} %param.37, f32[512,768]{1,0:T(8,128)} %fusion.7, bf16[5120,768]{1,0:T(8,128)(2,1)} %param.35, f32[5120]{0:T(1024)S(1)} %copy-done.23, f32[512]{0:T(512)S(1)} %add_rsqrt_fusion, bf16[512,1280]{1,0:T(8,128)(2,1)S(1)} %copy-done.4, ...), kind=kOutput, calls=%fused_computation.49 | convolution fusion | flops 8084258816 | bytes 33052672 | tf_op jit(solution)/shard_map/dot_general | solution.py:265
  314.8 65.7 %reduce-scatter.2.cloned.1.call-done = f32[32,5120]{1,0:T(8,128)} async-done(((f32[512,5120]{1,0:T(8,128)}), f32[32,5120]{1,0:T(8,128)}) %reduce-scatter.2.cloned.1.call-update) | async-done | bytes 655376 | tf_op jit(solution)/shard_map/reduce_scatter | solution.py:266
  380.6 1.9 add_convert_fusion
  (81 shorter events, 6.9 us)
Async XLA Ops:
  7.2 87.5 %copy-start = (bf16[32,256,64]{1,2,0:T(8,128)(2,1)S(1)}, bf16[32,256,64]{1,2,0:T(8,128)(2,1)}, u32[]{:S(2)}) copy-start(bf16[32,256,64]{1,2,0:T(8,128)(2,1)} %param.21) | copy-start | bytes 3145732
  7.2 8.6 %copy-start.3 = (bf16[32,5120]{1,0:T(8,128)(2,1)S(1)}, bf16[32,5120]{1,0:T(8,128)(2,1)}, u32[]{:S(2)}) copy-start(bf16[32,5120]{1,0:T(8,128)(2,1)} %x_ref.7) | copy-start | bytes 983044
  7.2 7.7 %copy-start.17 = (f32[32,32]{1,0:T(8,128)S(1)}, f32[32,32]{1,0:T(8,128)}, u32[]{:S(2)}) copy-start(f32[32,32]{1,0:T(8,128)} %param.23) | copy-start | bytes 12292
  7.2 7.7 %copy-start.18 = (f32[32,32]{1,0:T(8,128)S(1)}, f32[32,32]{1,0:T(8,128)}, u32[]{:S(2)}) copy-start(f32[32,32]{1,0:T(8,128)} %param.24) | copy-start | bytes 12292
  7.2 8.5 %copy-start.12 = (f32[5120]{0:T(1024)S(1)}, f32[5120]{0:T(1024)}, u32[]{:S(2)}) copy-start(f32[5120]{0:T(1024)} %param.25) | copy-start | bytes 61444
  7.2 175.9 %all-gather.11.cloned.1.call-start = ((), (), s32[]{:S(2)}) async-start(), calls=%async_computation.4 | async-start | bytes 1392640 | tf_op jit(solution)/shard_map/all_gather | solution.py:259
  15.6 77.1 %copy-start.14 = (bf16[32,32]{1,0:T(8,128)(2,1)}, bf16[32,32]{1,0:T(8,128)(2,1)S(1)}, u32[]{:S(2)}) copy-start(bf16[32,32]{1,0:T(8,128)(2,1)S(1)} %get-tuple-element.9) | copy-start | bytes 6148
  15.8 10.5 %copy-start.20 = (f32[1536]{0:T(1024)S(1)}, f32[1536]{0:T(1024)}, u32[]{:S(2)}) copy-start(f32[1536]{0:T(1024)} %param.27) | copy-start | bytes 18436
  27.3 38.5 %copy-start.22 = (s32[32]{0:T(128)S(1)}, s32[32]{0:T(128)}, u32[]{:S(2)}) copy-start(s32[32]{0:T(128)} %param.22) | copy-start | bytes 388
  27.3 39.2 %copy-start.21 = (f32[512]{0:T(512)S(1)}, f32[512]{0:T(512)}, u32[]{:S(2)}) copy-start(f32[512]{0:T(512)} %param.30) | copy-start | bytes 6148
  82.2 4.1 %copy-start.2 = (bf16[32,128,512]{2,1,0:T(8,128)(2,1)S(1)}, bf16[32,128,512]{2,1,0:T(8,128)(2,1)}, u32[]{:S(2)}) copy-start(bf16[32,128,512]{2,1,0:T(8,128)(2,1)} %absorb.1) | copy-start | bytes 12582916
  82.2 16.4 %slice-start = ((s8[8388608]{0:T(1024)(128)(4,1)}), s8[4194304]{0:T(1024)(128)(4,1)S(1)}, s32[]{:S(2)}) async-start(s8[8388608]{0:T(1024)(128)(4,1)} %bitcast.31), calls=%async_computation.6 | async-start | bytes 8388608
  86.3 12.2 %slice-start.1 = ((s8[8388608]{0:T(1024)(128)(4,1)}), s8[4194304]{0:T(1024)(128)(4,1)S(1)}, s32[]{:S(2)}) async-start(s8[8388608]{0:T(1024)(128)(4,1)} %bitcast.31), calls=%async_computation.7 | async-start | bytes 8388608
  94.7 2.4 copy-start.13
  94.7 3.8 copy-start.19
  133.0 76.5 %all-gather.9.cloned.1.call-start = ((), (), s32[]{:S(2)}) async-start(), calls=%async_computation.3 | async-start | bytes 1392640 | tf_op jit(solution)/shard_map/all_gather | solution.py:259
  149.6 95.6 %all-gather.5.cloned.1.call-start = ((), (), s32[]{:S(2)}) async-start(), calls=%async_computation.1 | async-start | bytes 1392640 | tf_op jit(solution)/shard_map/all_gather | solution.py:259
  166.4 114.4 %all-gather.7.cloned.1.call-start = ((), (), s32[]{:S(2)}) async-start(), calls=%async_computation.2 | async-start | bytes 1392640 | tf_op jit(solution)/shard_map/all_gather | solution.py:259
  182.9 101.9 %copy-start.23 = (f32[5120]{0:T(1024)S(1)}, f32[5120]{0:T(1024)}, u32[]{:S(2)}) copy-start(f32[5120]{0:T(1024)} %param.34) | copy-start | bytes 61444
  183.0 197.5 %reduce-scatter.2.cloned.1.call-start = ((), (), s32[]{:S(2)}) async-start(), calls=%async_computation.5 | async-start | bytes 11141120 | tf_op jit(solution)/shard_map/reduce_scatter | solution.py:266
  183.1 101.8 %copy-start.4 = (bf16[512,1280]{1,0:T(8,128)(2,1)S(1)}, bf16[512,1280]{1,0:T(8,128)(2,1)}, u32[]{:S(2)}) copy-start(bf16[512,1280]{1,0:T(8,128)(2,1)} %all-gather.11.cloned.1.call-done) | copy-start | bytes 3932164
  280.7 4.2 %copy-start.5 = (bf16[512,1280]{1,0:T(8,128)(2,1)S(1)}, bf16[512,1280]{1,0:T(8,128)(2,1)}, u32[]{:S(2)}) copy-start(bf16[512,1280]{1,0:T(8,128)(2,1)} %all-gather.9.cloned.1.call-done) | copy-start | bytes 3932164
  280.7 4.2 %copy-start.6 = (bf16[512,1280]{1,0:T(8,128)(2,1)S(1)}, bf16[512,1280]{1,0:T(8,128)(2,1)}, u32[]{:S(2)}) copy-start(bf16[512,1280]{1,0:T(8,128)(2,1)} %all-gather.5.cloned.1.call-done) | copy-start | bytes 3932164
  280.7 4.2 %copy-start.7 = (bf16[512,1280]{1,0:T(8,128)(2,1)S(1)}, bf16[512,1280]{1,0:T(8,128)(2,1)}, u32[]{:S(2)}) copy-start(bf16[512,1280]{1,0:T(8,128)(2,1)} %all-gather.7.cloned.1.call-done) | copy-start | bytes 3932164
  313.3 69.1 %copy-start.1 = (bf16[32,256,64]{1,2,0:T(8,128)(2,1)S(1)}, bf16[32,256,64]{1,2,0:T(8,128)(2,1)}, u32[]{:S(2)}) copy-start(bf16[32,256,64]{1,2,0:T(8,128)(2,1)} %param.21) | copy-start | bytes 3145732
  313.3 0.8 copy-start.15
  313.4 0.8 copy-start.16
  313.4 67.2 %copy-start.8 = (bf16[32,1280]{1,0:T(8,128)(2,1)S(1)}, bf16[32,1280]{1,0:T(8,128)(2,1)}, u32[]{:S(2)}) copy-start(bf16[32,1280]{1,0:T(8,128)(2,1)} %out_columns.7) | copy-start | bytes 245764
  313.4 67.2 %copy-start.9 = (bf16[32,1280]{1,0:T(8,128)(2,1)S(1)}, bf16[32,1280]{1,0:T(8,128)(2,1)}, u32[]{:S(2)}) copy-start(bf16[32,1280]{1,0:T(8,128)(2,1)} %out_columns.6) | copy-start | bytes 245764
  313.4 67.2 %copy-start.10 = (bf16[32,1280]{1,0:T(8,128)(2,1)S(1)}, bf16[32,1280]{1,0:T(8,128)(2,1)}, u32[]{:S(2)}) copy-start(bf16[32,1280]{1,0:T(8,128)(2,1)} %out_columns.4) | copy-start | bytes 245764
  313.4 67.2 %copy-start.11 = (bf16[32,1280]{1,0:T(8,128)(2,1)S(1)}, bf16[32,1280]{1,0:T(8,128)(2,1)}, u32[]{:S(2)}) copy-start(bf16[32,1280]{1,0:T(8,128)(2,1)} %out_columns.5) | copy-start | bytes 245764
Sparse Core Ops, SparseCore 0:
  133.2 40.5 all-gather.10
  175.4 34.0 all-gather.8
  211.1 34.0 all-gather.4
  246.7 33.9 all-gather.6
  313.6 66.9 reduce-scatter.1

commit v2 on v1

--- a/solution.py
+++ b/solution.py
@@ -1,3 +1,4 @@
+import functools
 import math
 import jax
 import jax.numpy as jnp
@@ -181,40 +182,206 @@
     )(lat_out, w_uv)
 
 
-def out_kernel(o_ref, x_ref, w_ref, r_ref, acc):
-    step = pl.program_id(0)
-
-    @pl.when(step == 0)
-    def _():
-        acc[...] = x_ref[...].astype(jnp.float32)
-
-    acc[...] += jnp.dot(o_ref[...], w_ref[...], preferred_element_type=jnp.float32)
-
-    @pl.when(step == pl.num_programs(0) - 1)
-    def _():
-        r_ref[...] = acc[...].astype(jnp.bfloat16)
-
-
-OUT_PARTS = 4
-OUT_DEPTH = 4096
-
-
-def out_columns(head_out, hidden, w_flat, part):
-    batch, depth = head_out.shape
-    columns = w_flat.shape[1] // OUT_PARTS
+def mlp_kernel(axis, chips, u_ref, r_ref, gate_hbm, up_hbm, down_hbm, o_ref, gate_w, up_w, down_w, rows_in, acts, ring, peer_out, peer_in, contrib, fin_in,
+               load_sem, ag_send, ag_recv, pe_send, pe_recv, rs_send, rs_recv, px_send, px_recv, fin_send, fin_recv):
+    me = lax.axis_index(axis)
+    core = lax.rem(me, 2)
+    other = 1 - core
+    chip = lax.div(me, 2)
+    peer = chip * 2 + other
+    ahead = lax.rem(chip + 1, chips) * 2 + core
+    behind = lax.rem(chip + chips - 1, chips) * 2 + core
+    sides = (ahead, behind)
+    half_way = chips // 2
+    width = u_ref.shape[-1]
+    quarter = width // 4
+    tile = 256
+    sub_rows = u_ref.shape[1]
+    own_rows = 2 * sub_rows
+    block_rows = 2 * own_rows
+    hidden = gate_w.shape[1]
+
+    loads = [pltpu.make_async_copy(src, dst, load_sem.at[n]) for n, (src, dst) in enumerate(((gate_hbm, gate_w), (up_hbm, up_w), (down_hbm, down_w)))]
+    for load in loads:
+        load.start()
+
+    barrier = pltpu.get_barrier_semaphore()
+    for device in (ahead, behind, peer):
+        pl.semaphore_signal(barrier, inc=1, device_id={axis: device}, device_id_type=pl.DeviceIdType.MESH)
+    pl.semaphore_wait(barrier, 3)
+
+    def remote(src, dst, send, recv, device):
+        return pltpu.make_async_remote_copy(src_ref=src, dst_ref=dst, send_sem=send, recv_sem=recv, device_id={axis: device}, device_id_type=pl.DeviceIdType.MESH)
+
+    def block_at(side, hop):
+        return hop if side == 0 else lax.rem(chips - hop, chips)
+
+    def hop_copy(side, hop, sub):
+        src = u_ref.at[sub] if isinstance(hop, int) and hop == 1 else rows_in.at[block_at(side, hop - 1), core, sub]
+        return remote(src, rows_in.at[block_at(side, hop), core, sub], ag_send.at[side, hop - 1, sub], ag_recv.at[side, hop - 1, sub], sides[side])
+
+    def peer_copy(block):
+        src = u_ref if isinstance(block, int) and block == 0 else rows_in.at[block, core]
+        return remote(src, rows_in.at[block, core], pe_send.at[block], pe_recv.at[block], peer)
+
+    for sub in range(2):
+        for side in range(2):
+            hop_copy(side, 1, sub).start()
+    peer_copy(0).start()
+    rows_in[0, core] = u_ref[...]
+    loads[0].wait()
+    loads[1].wait()
+
+    def gather_step(hop, carry):
+        last = hop == half_way
+        for sub in range(2):
+            for side in range(2):
+                def arrive(side=side, sub=sub):
+                    remote(rows_in.at[block_at(side, hop), core, sub], rows_in.at[block_at(side, hop), core, sub], ag_send.at[side, hop - 1, sub], ag_recv.at[side, hop - 1, sub], sides[side]).wait_recv()
+
+                def forward(side=side, sub=sub):
+                    hop_copy(side, hop + 1, sub).start()
+
+                if side == sub:
+                    arrive()
+                    pl.when(jnp.logical_not(last))(forward)
+                else:
+                    pl.when(jnp.logical_not(last))(arrive)
+                    pl.when(hop < half_way - 1)(forward)
+        first = hop
+        second = jnp.where(last, 0, chips - hop)
+        peer_copy(first).start()
+
+        @pl.when(jnp.logical_not(last))
+        def _():
+            peer_copy(second).start()
+
+        peer_copy(first).wait_recv()
+        peer_copy(second).wait_recv()
+        for_first = rows_in[first].reshape(block_rows, width)
+        for_second = rows_in[second].reshape(block_rows, width)
+        both = jnp.concatenate([for_first, for_second], axis=0)
+
+        def columns(n, carry):
+            at = pl.ds(pl.multiple_of(n * tile, tile), tile)
+            gate = jnp.dot(both, gate_w[:, at], preferred_element_type=jnp.float32)
+            up = jnp.dot(both, up_w[:, at], preferred_element_type=jnp.float32)
+            act = (jax.nn.silu(gate) * up).astype(jnp.bfloat16)
+            acts[first, :, at] = act[:block_rows]
+            acts[second, :, at] = act[block_rows:]
+            return carry
+
+        lax.fori_loop(0, hidden // tile, columns, 0)
+        return carry
+
+    lax.fori_loop(1, half_way + 1, gather_step, 0)
+    loads[2].wait()
+
+    def swap_copy(side, step):
+        return remote(peer_out.at[side, step], peer_in.at[side, step], px_send.at[side, step], px_recv.at[side, step], peer)
+
+    def ring_copy(side, step, sub):
+        return remote(ring.at[side, step, sub], ring.at[side, step + 1, sub], rs_send.at[side, step, sub], rs_recv.at[side, step, sub], sides[side])
+
+    def partial_sums(step):
+        blocks = (lax.rem(step + 1, chips), chips - 1 - step)
+        acted = [acts[block] for block in blocks]
+
+        def columns(n, carry):
+            at = pl.ds(pl.multiple_of(n * tile, tile), tile)
+            for side in range(2):
+                base = side * 2 * quarter + n * tile
+                kept = jnp.dot(acted[side], down_w[:, pl.ds(pl.multiple_of(base + core * quarter, 128), tile)], preferred_element_type=jnp.float32)
+                sent = jnp.dot(acted[side], down_w[:, pl.ds(pl.multiple_of(base + other * quarter, 128), tile)], preferred_element_type=jnp.float32)
+                contrib[side, :, :, at] = kept.reshape(2, own_rows, tile)
+                peer_out[side, step, :, :, at] = sent.reshape(2, own_rows, tile)
+            return carry
+
+        lax.fori_loop(0, quarter // tile, columns, 0)
+        for side in range(2):
+            swap_copy(side, step).start()
+
+    partial_sums(0)
+    for side in range(2):
+        swap_copy(side, 0).wait_recv()
+        for sub in range(2):
+            ring[side, 0, sub] = contrib[side, sub] + peer_in[side, 0, sub]
+            ring_copy(side, 0, sub).start()
+
+    def reduce_step(step, carry):
+        partial_sums(step)
+        for side in range(2):
+            swap_copy(side, step).wait_recv()
+        for sub in range(2):
+            for side in range(2):
+                ring_copy(side, step - 1, sub).wait_recv()
+                ring[side, step, sub] = ring[side, step, sub] + (contrib[side, sub] + peer_in[side, step, sub])
+                ring_copy(side, step, sub).start()
+        return carry
+
+    lax.fori_loop(1, chips - 1, reduce_step, 0)
+    final = chips - 1
+    partial_sums(final)
+    for side in range(2):
+        swap_copy(side, final).wait_recv()
+    for sub in range(2):
+        for side in range(2):
+            ring_copy(side, final - 1, sub).wait_recv()
+            ring[side, final, sub] = ring[side, final, sub] + (contrib[side, sub] + peer_in[side, final, sub])
+
+    def fin_copy(side):
+        return remote(ring.at[side, final, other], fin_in.at[side], fin_send.at[side], fin_recv.at[side], peer)
+
+    for side in range(2):
+        fin_copy(side).start()
+    for side in range(2):
+        mine = pl.ds(pl.multiple_of((2 * side + core) * quarter, 128), quarter)
+        o_ref[:, mine] = (r_ref[:, mine].astype(jnp.float32) + ring[side, final, core]).astype(jnp.bfloat16)
+    for side in range(2):
+        theirs = pl.ds(pl.multiple_of((2 * side + other) * quarter, 128), quarter)
+        fin_copy(side).wait_recv()
+        o_ref[:, theirs] = (r_ref[:, theirs].astype(jnp.float32) + fin_in[side]).astype(jnp.bfloat16)
+
+    for side in range(2):
+        fin_copy(side).wait_send()
+        for sub in range(2):
+            for hop in range(1, half_way + 1):
+                if hop < half_way or side == sub:
+                    hop_copy(side, hop, sub).wait_send()
+
+    def drain(step, carry):
+        for side in range(2):
+            swap_copy(side, step).wait_send()
+            for sub in range(2):
+                pl.when(step < final)(lambda side=side, sub=sub: ring_copy(side, step, sub).wait_send())
+        peer_copy(step).wait_send()
+        return carry
+
+    lax.fori_loop(0, chips, drain, 0)
+
+
+def mlp_group(axis, devices, mlp_in, residual, w_gate, w_up, w_down):
+    chips = devices // 2
+    rows, width = mlp_in.shape
+    hidden = w_gate.shape[1]
+    quarter = width // 4
+    dma = pltpu.SemaphoreType.DMA
+    any_spec = pl.BlockSpec(memory_space=pl.ANY)
+    vmem_spec = pl.BlockSpec(memory_space=pltpu.VMEM)
     return pl.pallas_call(
-        out_kernel,
-        grid=(depth // OUT_DEPTH,),
-        in_specs=[pl.BlockSpec((batch, OUT_DEPTH), lambda k: (0, k)),
-                  pl.BlockSpec((batch, columns), lambda k: (0, part)),
-                  pl.BlockSpec((OUT_DEPTH, columns), lambda k: (k, part))],
-        out_specs=pl.BlockSpec((batch, columns), lambda k: (0, 0)),
-        out_shape=jax.ShapeDtypeStruct((batch, columns), jnp.bfloat16),
-        scratch_shapes=[pltpu.VMEM((batch, columns), jnp.float32)],
-        compiler_params=pltpu.CompilerParams(vmem_limit_bytes=VMEM_BYTES),
-        cost_estimate=pl.CostEstimate(flops=2 * batch * depth * columns * 16, bytes_accessed=2 * depth * columns, transcendentals=0),
-        name='out_columns',
-    )(head_out, hidden, w_flat)
+        functools.partial(mlp_kernel, axis, chips),
+        in_specs=[vmem_spec, vmem_spec, any_spec, any_spec, any_spec],
+        out_specs=vmem_spec,
+        out_shape=jax.ShapeDtypeStruct((rows, width), jnp.bfloat16),
+        scratch_shapes=[pltpu.VMEM((width, hidden), jnp.bfloat16), pltpu.VMEM((width, hidden), jnp.bfloat16), pltpu.VMEM((hidden, width), jnp.bfloat16),
+                        pltpu.VMEM((chips, 2, 2, rows // 2, width), jnp.bfloat16), pltpu.VMEM((chips, 2 * rows, hidden), jnp.bfloat16),
+                        pltpu.VMEM((2, chips, 2, rows, quarter), jnp.float32), pltpu.VMEM((2, chips, 2, rows, quarter), jnp.float32),
+                        pltpu.VMEM((2, chips, 2, rows, quarter), jnp.float32), pltpu.VMEM((2, 2, rows, quarter), jnp.float32), pltpu.VMEM((2, rows, quarter), jnp.float32),
+                        dma((3,)), dma((2, chips // 2, 2)), dma((2, chips // 2, 2)), dma((chips,)), dma((chips,)),
+                        dma((2, chips, 2)), dma((2, chips, 2)), dma((2, chips)), dma((2, chips)), dma((2,)), dma((2,))],
+        compiler_params=pltpu.CompilerParams(collective_id=0, has_side_effects=True, vmem_limit_bytes=VMEM_BYTES),
+        name='mlp_group',
+    )(mlp_in.reshape(2, rows // 2, width), residual, w_gate, w_up, w_down)
 
 
 def attention_rows(hidden, ckv_cache, kpe_cache, cache_len, rope_cos, rope_sin, norm_attn, w_dq, norm_q, w_uq, w_dkv, norm_kv, w_uk, w_uv, w_out):
@@ -241,9 +408,9 @@
                 + exp_new.astype(jnp.bfloat16).astype(jnp.float32)[..., None] * ckv_new.astype(jnp.float32)[:, None, :])
     lat_out = (weighted / norm_sum[..., None]).astype(jnp.bfloat16)
     head_out = value_heads(lat_out, w_uv)
-    w_flat = w_out.reshape(w_out.shape[0] * w_out.shape[1], w_out.shape[2])
-    parts = [out_columns(head_out, hidden, w_flat, part) for part in range(OUT_PARTS)]
-    return parts, ckv_new, kpe_new
+    attn_out = jnp.dot(head_out, w_out.reshape(w_out.shape[0] * w_out.shape[1], w_out.shape[2]), preferred_element_type=jnp.float32)
+    residual = (hidden.astype(jnp.float32) + attn_out).astype(jnp.bfloat16)
+    return residual, ckv_new, kpe_new
 
 
 def solution(mesh):
@@ -255,16 +422,9 @@
                 P(None, 'dp'), P(None, 'dp'), P('dp', None))
 
     def local_step(hidden, ckv_cache, kpe_cache, cache_len, rope_cos, rope_sin, norm_attn, w_dq, norm_q, w_uq, w_dkv, norm_kv, w_uk, w_uv, w_out, norm_mlp, w_gate, w_up, w_down):
-        parts, ckv_new, kpe_new = attention_rows(hidden, ckv_cache, kpe_cache, cache_len, rope_cos, rope_sin, norm_attn, w_dq, norm_q, w_uq, w_dkv, norm_kv, w_uk, w_uv, w_out)
-        gathered = [lax.all_gather(part, 'dp', axis=0, tiled=True) for part in parts]
-        residual = jnp.concatenate(parts, axis=1)
-        group_in = rms_norm(jnp.concatenate(gathered, axis=1), norm_mlp).astype(jnp.bfloat16)
-        gate_val = jnp.dot(group_in, w_gate, preferred_element_type=jnp.float32)
-        up_val = jnp.dot(group_in, w_up, preferred_element_type=jnp.float32)
-        act_val = (jax.nn.silu(gate_val) * up_val).astype(jnp.bfloat16)
-        partial_sum = jnp.dot(act_val, w_down, preferred_element_type=jnp.float32)
-        mlp_rows = lax.psum_scatter(partial_sum, 'dp', scatter_dimension=0, tiled=True)
-        out_hidden = (residual.astype(jnp.float32) + mlp_rows).astype(jnp.bfloat16)
+        residual, ckv_new, kpe_new = attention_rows(hidden, ckv_cache, kpe_cache, cache_len, rope_cos, rope_sin, norm_attn, w_dq, norm_q, w_uq, w_dkv, norm_kv, w_uk, w_uv, w_out)
+        mlp_in = rms_norm(residual, norm_mlp).astype(jnp.bfloat16)
+        out_hidden = mlp_group('dp', mesh.shape['dp'], mlp_in, residual, w_gate, w_up, w_down)
         return out_hidden, ckv_new, kpe_new
 
     return jax.shard_map(local_step, mesh=mesh, in_specs=in_specs, out_specs=(row_spec, row_spec, row_spec), check_vma=False)

time: 391 us -> 265 us (0.68)
  waiting for transfers between devices: 164 us -> 0 us
  Pallas kernels: 125 us -> 159 us
  matrix products: 59.9 us -> 84.7 us
  between operations: 14.1 us -> 0.93 us
  other arithmetic: 13.9 us -> 7.54 us
    all_gather x4 -> x0, waiting for transfers between devices: 97.6 us -> none  [local_step(): lax.all_gather(part, 'dp', axis=0, tiled=True)]
    reduce_scatter x1 -> x0, waiting for transfers between devices: 65.7 us -> none  [local_step(): lax.psum_scatter(partial_sum, 'dp', scatter_dimension=0, tiled=True)]
    pallas_call x4 -> x1, Pallas kernels: 66 us -> 100 us  [mlp_group(): pl.pallas_call(functools.partial(mlp_kernel, axis, chips), in_specs=[vmem...]
    dot_general x2 -> x1, matrix products: 28.4 us -> 53.6 us  [attention_rows(): jnp.dot(head_out, w_out.reshape(w_out.shape[0] * w_out.shape[1], w_out.sh...]
    reduce_sum x3 -> x2, other arithmetic: 5.48 us -> 1.37 us  [rms_norm(): mean_sq = jnp.mean(floats * floats, axis=-1, keepdims=True)]
  transfers between devices with their start and end apart: 5 -> 0, of which waited for: 4 -> 0; matrix products, arithmetic and copies ran while one was open for 0% -> 0% of each run, Pallas kernels for 13% -> 0%
where the time goes in v2:
time: 265 us; the launch traced here: 264 us
  Pallas kernels  159 us (60%)
  matrix products  84.7 us (32%)
  local copies, waits for them, and re-layouts  11.7 us (4%)
  other arithmetic  7.54 us (3%)
    pallas_call x1, Pallas kernels, mlp_group(): pl.pallas_call(functools.partial(mlp_kernel, axis, chips), in_specs=[vmem...  100 us
    dot_general x1, matrix products, attention_rows(): jnp.dot(head_out, w_out.reshape(w_out.shape[0] * w_out.shape[1], w_out.sh...  53.6 us
    pallas_call x1, Pallas kernels, q_project(): pl.pallas_call(q_kernel, grid=(steps,), in_specs=[pl.BlockSpec((rows, dep...  31.8 us
    pallas_call x1, Pallas kernels, value_heads(): pl.pallas_call(value_kernel, grid=(heads // (HEAD_PACK * GROUP),), in_spe...  13.8 us
    pallas_call x1, Pallas kernels, absorb(): pl.pallas_call(absorb_kernel, grid=(heads // (HEAD_PACK * GROUP),), in_sp...  13.3 us
    dot_general x1, matrix products, attention_rows(): jnp.dot(normed, w_dq, preferred_element_type=jnp.float32)  8.46 us
    dot_general x1, matrix products, attention_rows(): jnp.einsum('bhl,btl->bht', q_abs, ckv_cache, preferred_element_type=jnp.f...  6.36 us

profile of v2, /device:TPU:21, one launch (start us, length us, event | category | flops | bytes accessed | tf_op | source)
XLA Modules:
  0.0 264.2 jit_solution(3732017609930532471)
XLA Ops:
  0.7 1.2 fusion.8
  2.0 0.7 iota_compare_fusion
  2.7 0.8 copy.26
  3.5 0.8 copy.28
  4.4 4.6 %fusion.12 = f32[32,576]{1,0:T(8,128)S(1)} fusion(bf16[5120,576]{0,1:T(8,128)(2,1)} %param.29, bf16[32,5120]{1,0:T(8,128)(2,1)} %param.19, f32[5120]{0:T(1024)} %param.25, f32[32]{0:T(128)S(1)} %add_rsqrt_fusion.3), kind=kOutput, calls=%fused_computation.24 | convolution fusion | flops 189399040 | bytes 6320256 | tf_op jit(solution)/shard_map/dot_general | solution.py:393
  9.1 0.1 multiply_reduce_fusion.1
  9.3 0.1 fusion.35
  9.4 0.7 pad_maximum_fusion.3
  10.1 0.7 fusion.23
  10.8 8.5 %multiply_reduce_fusion = (f32[32]{0:T(128)S(1)}, f32[32,1536]{1,0:T(8,128)S(1)}) fusion(bf16[5120,1536]{1,0:T(8,128)(2,1)} %param.26, bf16[32,5120]{1,0:T(8,128)(2,1)S(1)} %copy-done.3, f32[5120]{0:T(1024)S(1)} %copy-done.9, f32[32]{0:T(128)S(1)} %add_rsqrt_fusion.3), kind=kOutput, calls=%fused_computation.23 | convolution fusion | flops 504070112 | bytes 16273664 | tf_op jit(solution)/shard_map/dot_general | solution.py:391
  19.3 0.1 multiply_convert_fusion
  19.4 1.0 reshape.100.cos_ref
  20.4 1.0 reshape.101.sin_ref
  21.3 0.9 broadcast_bitcast_fusion.cq_ref
  22.3 31.8 %q_project.1 = (bf16[32,96,128]{2,1,0:T(8,128)(2,1)}, bf16[32,96,128]{2,1,0:T(8,128)(2,1)}) custom-call(bf16[256,1536]{1,0:T(8,128)(2,1)} %broadcast_bitcast_fusion.cq_ref, f32[4,256,1]{2,1,0:T(8,128)} %reshape.100.cos_ref, f32[4,256,1]{2,1,0:T(8,128)} %reshape.101.sin_ref, bf16[1536,192,128]{2,1,0:T(8,128)(2,1)} %bitcast.5.wa_ref.wb_ref, ...), custom_call_target="tpu_custom_call" | custom-call | flops 2415919104 | bytes 75497472 | tf_op jit(solution)/shard_map/q_project/pallas_call | solution.py:93
  54.1 1.0 slice.26
  55.0 1.1 slice.27
  56.1 0.9 fusion.11
  57.0 1.6 copy.33
  58.6 1.6 copy.32
  60.2 1.6 maximum_bitcast_fusion.q_ref
  61.7 13.3 %absorb.1 = bf16[32,128,512]{2,1,0:T(8,128)(2,1)} custom-call(bf16[32,128,128]{2,1,0:T(8,128)(2,1)} %maximum_bitcast_fusion.q_ref, bf16[512,128,128]{2,1,0:T(8,128)(2,1)} %w_ref.2), custom_call_target="tpu_custom_call" | custom-call | flops 536870912 | bytes 16777216 | tf_op jit(solution)/shard_map/absorb/pallas_call | solution.py:134
  75.0 4.1 %fusion.16 = f32[32,1,128]{2,1,0:T(1,128)} fusion(bf16[32,128,512]{2,1,0:T(8,128)(2,1)} %absorb.1, bf16[32,512,1]{1,0,2:T(8,128)(2,1)S(1)} %bitcast.36), kind=kOutput, calls=%fused_computation.26 | convolution fusion | flops 4194304 | bytes 4243456 | tf_op jit(solution)/shard_map/bhl,bl->bh/dot_general | solution.py:401
  79.2 6.4 %fusion.25 = f32[32,128,256]{2,1,0:T(8,128)S(1)} fusion(bf16[32,128,512]{2,1,0:T(8,128)(2,1)S(1)} %copy-done.2, bf16[32,256,512]{2,1,0:T(8,128)(2,1)} %param.20), kind=kOutput, calls=%fused_computation.48 | convolution fusion | flops 1073741824 | bytes 16777216 | tf_op jit(solution)/shard_map/bhl,btl->bht/dot_general | solution.py:397
  85.6 2.4 fusion.24
  88.0 1.3 fusion.1
  89.4 4.3 %divide_convert_fusion.l_ref = bf16[32,128,512]{2,1,0:T(8,128)(2,1)} fusion(f32[32,128]{1,0:T(8,128)S(1)} %get-tuple-element.12, f32[32,512]{1,0:T(8,128)S(1)} %copy-done.13, f32[32,128]{1,0:T(8,128)S(1)} %get-tuple-element.11, bf16[32,256,512]{2,1,0:T(8,128)(2,1)S(1)} %bitcast.32, f32[32,128,256]{2,1,0:T(8,128)S(1)} %get-tuple-element.16, ...), kind=kOutput, calls=%fused_computation | convolution fusion | flops 1084227584 | bytes 16891904 | tf_op jit(solution)/shard_map/bht,btl->bhl/dot_general | solution.py:407
  93.7 13.8 %value_heads.1 = bf16[32,16384]{1,0:T(8,128)(2,1)} custom-call(bf16[32,128,512]{2,1,0:T(8,128)(2,1)} %divide_convert_fusion.l_ref, bf16[512,128,128]{2,1,0:T(8,128)(2,1)} %w_ref.3), custom_call_target="tpu_custom_call" | custom-call | flops 536870912 | bytes 16777216 | tf_op jit(solution)/shard_map/value_heads/pallas_call | solution.py:171
  107.5 53.6 %fusion.5 = (f32[32]{0:T(128)S(1)}, bf16[32,5120]{1,0:T(8,128)(2,1)S(1)}) fusion(bf16[32,16384]{1,0:T(8,128)(2,1)} %value_heads.1, bf16[16384,5120]{1,0:T(8,128)(2,1)} %bitcast.13, bf16[32,5120]{1,0:T(8,128)(2,1)S(1)} %copy-done.4), kind=kOutput, calls=%fused_computation.13 | convolution fusion | flops 5369692160 | bytes 169476224 | tf_op jit(solution)/shard_map/dot_general | solution.py:411
  161.1 0.9 fusion.7
  162.0 100.5 %mlp_group.1 = bf16[32,5120]{1,0:T(8,128)(2,1)} custom-call(bf16[2,16,5120]{2,1,0:T(8,128)(2,1)} %bitcast.35, bf16[32,5120]{1,0:T(8,128)(2,1)} %copy-done.5, bf16[5120,768]{1,0:T(8,128)(2,1)} %gate_hbm.1, bf16[5120,768]{1,0:T(8,128)(2,1)} %up_hbm.1, bf16[768,5120]{1,0:T(8,128)(2,1)} %down_hbm.1), custom_call_target="tpu_custom_call" | custom-call | tf_op jit(solution)/shard_map/mlp_group/pallas_call | solution.py:371
  262.5 1.7 copy.43
  (50 shorter events, 0.4 us)
Async XLA Ops:
  0.6 84.9 %copy-start = (bf16[32,256,64]{1,2,0:T(8,128)(2,1)S(1)}, bf16[32,256,64]{1,2,0:T(8,128)(2,1)}, u32[]{:S(2)}) copy-start(bf16[32,256,64]{1,2,0:T(8,128)(2,1)} %param.21) | copy-start | bytes 3145732
  0.6 10.1 %copy-start.3 = (bf16[32,5120]{1,0:T(8,128)(2,1)S(1)}, bf16[32,5120]{1,0:T(8,128)(2,1)}, u32[]{:S(2)}) copy-start(bf16[32,5120]{1,0:T(8,128)(2,1)} %param.19) | copy-start | bytes 983044
  0.7 10.1 %copy-start.9 = (f32[5120]{0:T(1024)S(1)}, f32[5120]{0:T(1024)}, u32[]{:S(2)}) copy-start(f32[5120]{0:T(1024)} %param.25) | copy-start | bytes 61444
  0.7 8.5 %copy-start.12 = (f32[32,32]{1,0:T(8,128)S(1)}, f32[32,32]{1,0:T(8,128)}, u32[]{:S(2)}) copy-start(f32[32,32]{1,0:T(8,128)} %param.24) | copy-start | bytes 12292
  0.7 8.5 %copy-start.11 = (f32[32,32]{1,0:T(8,128)S(1)}, f32[32,32]{1,0:T(8,128)}, u32[]{:S(2)}) copy-start(f32[32,32]{1,0:T(8,128)} %param.23) | copy-start | bytes 12292
  0.7 9.4 %copy-start.17 = (f32[512]{0:T(512)S(1)}, f32[512]{0:T(512)}, u32[]{:S(2)}) copy-start(f32[512]{0:T(512)} %param.30) | copy-start | bytes 6148
  10.8 64.3 %copy-start.8 = (bf16[32,512]{1,0:T(8,128)(2,1)}, bf16[32,512]{1,0:T(8,128)(2,1)S(1)}, u32[]{:S(2)}) copy-start(bf16[32,512]{1,0:T(8,128)(2,1)S(1)} %get-tuple-element.23) | copy-start | bytes 98308
  10.8 8.5 %copy-start.16 = (f32[1536]{0:T(1024)S(1)}, f32[1536]{0:T(1024)}, u32[]{:S(2)}) copy-start(f32[1536]{0:T(1024)} %param.27) | copy-start | bytes 18436
  55.0 1.9 copy-start.6
  56.1 0.9 copy-start.7
  75.0 4.1 %copy-start.2 = (bf16[32,128,512]{2,1,0:T(8,128)(2,1)S(1)}, bf16[32,128,512]{2,1,0:T(8,128)(2,1)}, u32[]{:S(2)}) copy-start(bf16[32,128,512]{2,1,0:T(8,128)(2,1)} %absorb.1) | copy-start | bytes 12582916
  79.2 10.2 %slice-start = ((s8[8388608]{0:T(1024)(128)(4,1)}), s8[4194304]{0:T(1024)(128)(4,1)S(1)}, s32[]{:S(2)}) async-start(s8[8388608]{0:T(1024)(128)(4,1)} %bitcast.31), calls=%async_computation | async-start | bytes 8388608
  79.2 10.2 %slice-start.1 = ((s8[8388608]{0:T(1024)(128)(4,1)}), s8[4194304]{0:T(1024)(128)(4,1)S(1)}, s32[]{:S(2)}) async-start(s8[8388608]{0:T(1024)(128)(4,1)} %bitcast.31), calls=%async_computation.1 | async-start | bytes 8388608
  85.6 2.4 copy-start.10
  85.6 2.4 copy-start.14
  88.0 1.4 copy-start.13
  93.7 13.8 %copy-start.4 = (bf16[32,5120]{1,0:T(8,128)(2,1)S(1)}, bf16[32,5120]{1,0:T(8,128)(2,1)}, u32[]{:S(2)}) copy-start(bf16[32,5120]{1,0:T(8,128)(2,1)} %param.19) | copy-start | bytes 983044
  107.5 53.6 %copy-start.15 = (f32[5120]{0:T(1024)S(1)}, f32[5120]{0:T(1024)}, u32[]{:S(2)}) copy-start(f32[5120]{0:T(1024)} %param.34) | copy-start | bytes 61444
  161.1 0.9 copy-start.5
  162.0 102.2 %copy-start.1 = (bf16[32,256,64]{1,2,0:T(8,128)(2,1)S(1)}, bf16[32,256,64]{1,2,0:T(8,128)(2,1)}, u32[]{:S(2)}) copy-start(bf16[32,256,64]{1,2,0:T(8,128)(2,1)} %param.21) | copy-start | bytes 3145732

commit v3 on v2

--- a/solution.py
+++ b/solution.py
@@ -229,8 +229,55 @@
             hop_copy(side, 1, sub).start()
     peer_copy(0).start()
     rows_in[0, core] = u_ref[...]
-    loads[0].wait()
-    loads[1].wait()
+    for load in loads:
+        load.wait()
+
+    final = chips - 1
+
+    def swap_copy(side, step):
+        return remote(peer_out.at[side, step], peer_in.at[side, step], px_send.at[side, step], px_recv.at[side, step], peer)
+
+    def ring_copy(side, step, sub):
+        return remote(ring.at[side, step, sub], ring.at[side, step + 1, sub], rs_send.at[side, step, sub], rs_recv.at[side, step, sub], sides[side])
+
+    def partial_sums(step):
+        blocks = (lax.rem(step + 1, chips), chips - 1 - step)
+        acted = [acts[block] for block in blocks]
+
+        def columns(n, carry):
+            at = pl.ds(pl.multiple_of(n * tile, tile), tile)
+            for side in range(2):
+                base = side * 2 * quarter + n * tile
+                kept = jnp.dot(acted[side], down_w[:, pl.ds(pl.multiple_of(base + core * quarter, 128), tile)], preferred_element_type=jnp.float32)
+                sent = jnp.dot(acted[side], down_w[:, pl.ds(pl.multiple_of(base + other * quarter, 128), tile)], preferred_element_type=jnp.float32)
+                contrib[side, :, :, at] = kept.reshape(2, own_rows, tile)
+                peer_out[side, step, :, :, at] = sent.reshape(2, own_rows, tile)
+            return carry
+
+        lax.fori_loop(0, quarter // tile, columns, 0)
+        for side in range(2):
+            swap_copy(side, step).start()
+
+    def reduce_step(step):
+        partial_sums(step)
+        for side in range(2):
+            swap_copy(side, step).wait_recv()
+        for sub in range(2):
+            for side in range(2):
+                added = contrib[side, sub] + peer_in[side, step, sub]
+
+                @pl.when(step == 0)
+                def _(side=side, sub=sub, added=added):
+                    ring[side, step, sub] = added
+
+                @pl.when(step > 0)
+                def _(side=side, sub=sub, added=added):
+                    ring_copy(side, step - 1, sub).wait_recv()
+                    ring[side, step, sub] = ring[side, step, sub] + added
+
+                @pl.when(step < final)
+                def _(side=side, sub=sub):
+                    ring_copy(side, step, sub).start()
 
     def gather_step(hop, carry):
         last = hop == half_way
@@ -272,62 +319,16 @@
             return carry
 
         lax.fori_loop(0, hidden // tile, columns, 0)
+        reduce_step(hop - 1)
         return carry
 
     lax.fori_loop(1, half_way + 1, gather_step, 0)
-    loads[2].wait()
-
-    def swap_copy(side, step):
-        return remote(peer_out.at[side, step], peer_in.at[side, step], px_send.at[side, step], px_recv.at[side, step], peer)
-
-    def ring_copy(side, step, sub):
-        return remote(ring.at[side, step, sub], ring.at[side, step + 1, sub], rs_send.at[side, step, sub], rs_recv.at[side, step, sub], sides[side])
-
-    def partial_sums(step):
-        blocks = (lax.rem(step + 1, chips), chips - 1 - step)
-        acted = [acts[block] for block in blocks]
-
-        def columns(n, carry):
-            at = pl.ds(pl.multiple_of(n * tile, tile), tile)
-            for side in range(2):
-                base = side * 2 * quarter + n * tile
-                kept = jnp.dot(acted[side], down_w[:, pl.ds(pl.multiple_of(base + core * quarter, 128), tile)], preferred_element_type=jnp.float32)
-                sent = jnp.dot(acted[side], down_w[:, pl.ds(pl.multiple_of(base + other * quarter, 128), tile)], preferred_element_type=jnp.float32)
-                contrib[side, :, :, at] = kept.reshape(2, own_rows, tile)
-                peer_out[side, step, :, :, at] = sent.reshape(2, own_rows, tile)
-            return carry
-
-        lax.fori_loop(0, quarter // tile, columns, 0)
-        for side in range(2):
-            swap_copy(side, step).start()
-
-    partial_sums(0)
-    for side in range(2):
-        swap_copy(side, 0).wait_recv()
-        for sub in range(2):
-            ring[side, 0, sub] = contrib[side, sub] + peer_in[side, 0, sub]
-            ring_copy(side, 0, sub).start()
-
-    def reduce_step(step, carry):
-        partial_sums(step)
-        for side in range(2):
-            swap_copy(side, step).wait_recv()
-        for sub in range(2):
-            for side in range(2):
-                ring_copy(side, step - 1, sub).wait_recv()
-                ring[side, step, sub] = ring[side, step, sub] + (contrib[side, sub] + peer_in[side, step, sub])
-                ring_copy(side, step, sub).start()
+
+    def later_step(step, carry):
+        reduce_step(step)
         return carry
 
-    lax.fori_loop(1, chips - 1, reduce_step, 0)
-    final = chips - 1
-    partial_sums(final)
-    for side in range(2):
-        swap_copy(side, final).wait_recv()
-    for sub in range(2):
-        for side in range(2):
-            ring_copy(side, final - 1, sub).wait_recv()
-            ring[side, final, sub] = ring[side, final, sub] + (contrib[side, sub] + peer_in[side, final, sub])
+    lax.fori_loop(half_way, chips, later_step, 0)
 
     def fin_copy(side):
         return remote(ring.at[side, final, other], fin_in.at[side], fin_send.at[side], fin_recv.at[side], peer)
@@ -384,7 +385,90 @@
     )(mlp_in.reshape(2, rows // 2, width), residual, w_gate, w_up, w_down)
 
 
-def attention_rows(hidden, ckv_cache, kpe_cache, cache_len, rope_cos, rope_sin, norm_attn, w_dq, norm_q, w_uq, w_dkv, norm_kv, w_uk, w_uv, w_out):
+def pair_kernel(axis, eps, o_ref, x_ref, g_ref, w_hbm, r_ref, u_ref, o_all, x_in, r_out, r_in, acc, stream, load_sem, send_sem, recv_sem):
+    me = lax.axis_index(axis)
+    core = lax.rem(me, 2)
+    other = 1 - core
+    peer = me + 1 - 2 * core
+    rows, width = x_ref.shape
+    half = width // 2
+    slots, depth = stream.shape[0], stream.shape[1]
+    count = o_ref.shape[1] // depth
+    mine = pl.ds(pl.multiple_of(core * half, 128), half)
+    theirs = pl.ds(pl.multiple_of(other * half, 128), half)
+
+    def load(step):
+        slot = lax.rem(step, slots)
+        return pltpu.make_async_copy(w_hbm.at[pl.ds(pl.multiple_of(step * depth, depth), depth), mine], stream.at[slot], load_sem.at[slot])
+
+    for step in range(slots):
+        load(step).start()
+    barrier = pltpu.get_barrier_semaphore()
+    pl.semaphore_signal(barrier, inc=1, device_id={axis: peer}, device_id_type=pl.DeviceIdType.MESH)
+    pl.semaphore_wait(barrier, 1)
+
+    def remote(src, dst, n):
+        return pltpu.make_async_remote_copy(src_ref=src, dst_ref=dst, send_sem=send_sem.at[n], recv_sem=recv_sem.at[n], device_id={axis: peer}, device_id_type=pl.DeviceIdType.MESH)
+
+    o_copy = remote(o_ref, o_all.at[core], 0)
+    x_copy = remote(x_ref.at[:, theirs], x_in, 1)
+    o_copy.start()
+    x_copy.start()
+    o_all[core] = o_ref[...]
+    acc[...] = jnp.zeros_like(acc)
+    o_copy.wait_recv()
+
+    def body(step, carry):
+        load(step).wait()
+        heads = o_all[:, :, pl.ds(pl.multiple_of(step * depth, depth), depth)].reshape(2 * rows, depth)
+        acc[...] += jnp.dot(heads, stream[lax.rem(step, slots)], preferred_element_type=jnp.float32).reshape(2, rows, half)
+
+        @pl.when(step + slots < count)
+        def _():
+            load(step + slots).start()
+
+        return carry
+
+    lax.fori_loop(0, count, body, 0)
+    x_copy.wait_recv()
+    r_out[...] = (x_in[...].astype(jnp.float32) + acc[other]).astype(jnp.bfloat16)
+    r_copy = remote(r_out, r_in, 2)
+    r_copy.start()
+    r_ref[:, mine] = (x_ref[:, mine].astype(jnp.float32) + acc[core]).astype(jnp.bfloat16)
+    r_copy.wait_recv()
+    r_ref[:, theirs] = r_in[...]
+    whole = r_ref[...].astype(jnp.float32)
+    mean_sq = jnp.mean(whole * whole, axis=-1, keepdims=True)
+    u_ref[...] = (whole * lax.rsqrt(mean_sq + eps) * g_ref[...]).astype(jnp.bfloat16)
+    o_copy.wait_send()
+    x_copy.wait_send()
+    r_copy.wait_send()
+
+
+OUT_DEPTH = 1024
+OUT_SLOTS = 4
+
+
+def pair_out(axis, head_out, hidden, w_flat, norm_mlp):
+    rows, depth = head_out.shape
+    width = hidden.shape[1]
+    half = width // 2
+    dma = pltpu.SemaphoreType.DMA
+    vmem_spec = pl.BlockSpec(memory_space=pltpu.VMEM)
+    return pl.pallas_call(
+        functools.partial(pair_kernel, axis, EPSILON),
+        in_specs=[vmem_spec, vmem_spec, vmem_spec, pl.BlockSpec(memory_space=pl.ANY)],
+        out_specs=[vmem_spec, vmem_spec],
+        out_shape=[jax.ShapeDtypeStruct((rows, width), jnp.bfloat16)] * 2,
+        scratch_shapes=[pltpu.VMEM((2, rows, depth), jnp.bfloat16), pltpu.VMEM((rows, half), jnp.bfloat16), pltpu.VMEM((rows, half), jnp.bfloat16),
+                        pltpu.VMEM((rows, half), jnp.bfloat16), pltpu.VMEM((2, rows, half), jnp.float32), pltpu.VMEM((OUT_SLOTS, OUT_DEPTH, half), jnp.bfloat16),
+                        dma((OUT_SLOTS,)), dma((3,)), dma((3,))],
+        compiler_params=pltpu.CompilerParams(collective_id=1, has_side_effects=True, vmem_limit_bytes=VMEM_BYTES),
+        name='pair_out',
+    )(head_out, hidden, norm_mlp[None, :], w_flat)
+
+
+def attention_rows(axis, hidden, ckv_cache, kpe_cache, cache_len, rope_cos, rope_sin, norm_attn, w_dq, norm_q, w_uq, w_dkv, norm_kv, w_uk, w_uv, w_out, norm_mlp):
     value_a7 = w_uk.shape[0]
     score_scale = MSCALE * MSCALE / math.sqrt(w_uq.shape[2])
     normed = rms_norm(hidden, norm_attn).astype(jnp.bfloat16)
@@ -408,9 +492,9 @@
                 + exp_new.astype(jnp.bfloat16).astype(jnp.float32)[..., None] * ckv_new.astype(jnp.float32)[:, None, :])
     lat_out = (weighted / norm_sum[..., None]).astype(jnp.bfloat16)
     head_out = value_heads(lat_out, w_uv)
-    attn_out = jnp.dot(head_out, w_out.reshape(w_out.shape[0] * w_out.shape[1], w_out.shape[2]), preferred_element_type=jnp.float32)
-    residual = (hidden.astype(jnp.float32) + attn_out).astype(jnp.bfloat16)
-    return residual, ckv_new, kpe_new
+    w_flat = w_out.reshape(w_out.shape[0] * w_out.shape[1], w_out.shape[2])
+    residual, mlp_in = pair_out(axis, head_out, hidden, w_flat, norm_mlp)
+    return residual, mlp_in, ckv_new, kpe_new
 
 
 def solution(mesh):
@@ -422,8 +506,7 @@
                 P(None, 'dp'), P(None, 'dp'), P('dp', None))
 
     def local_step(hidden, ckv_cache, kpe_cache, cache_len, rope_cos, rope_sin, norm_attn, w_dq, norm_q, w_uq, w_dkv, norm_kv, w_uk, w_uv, w_out, norm_mlp, w_gate, w_up, w_down):
-        residual, ckv_new, kpe_new = attention_rows(hidden, ckv_cache, kpe_cache, cache_len, rope_cos, rope_sin, norm_attn, w_dq, norm_q, w_uq, w_dkv, norm_kv, w_uk, w_uv, w_out)
-        mlp_in = rms_norm(residual, norm_mlp).astype(jnp.bfloat16)
+        residual, mlp_in, ckv_new, kpe_new = attention_rows('dp', hidden, ckv_cache, kpe_cache, cache_len, rope_cos, rope_sin, norm_attn, w_dq, norm_q, w_uq, w_dkv, norm_kv, w_uk, w_uv, w_out, norm_mlp)
         out_hidden = mlp_group('dp', mesh.shape['dp'], mlp_in, residual, w_gate, w_up, w_down)
         return out_hidden, ckv_new, kpe_new
 

time: 265 us -> 237 us (0.89)
  matrix products: 84.7 us -> 31.1 us
  Pallas kernels: 159 us -> 186 us
    dot_general x1 -> x0, matrix products: 53.6 us -> none  [attention_rows(): jnp.dot(head_out, w_out.reshape(w_out.shape[0] * w_out.shape[1], w_out.sh...]
    pallas_call x0 -> x1, Pallas kernels: none -> 35 us  [pair_out(): pl.pallas_call(functools.partial(pair_kernel, axis, EPSILON), in_specs=[v...]
    pallas_call x1, Pallas kernels: 100 us -> 92.1 us  [mlp_group(): pl.pallas_call(functools.partial(mlp_kernel, axis, chips), in_specs=[vmem...]
where the time goes in v3:
time: 237 us; the launch traced here: 236 us
  Pallas kernels  186 us (78%)
  matrix products  31.1 us (13%)
  local copies, waits for them, and re-layouts  11.7 us (5%)
  other arithmetic  6.66 us (3%)
    pallas_call x1, Pallas kernels, mlp_group(): pl.pallas_call(functools.partial(mlp_kernel, axis, chips), in_specs=[vmem...  92.1 us
    pallas_call x1, Pallas kernels, pair_out(): pl.pallas_call(functools.partial(pair_kernel, axis, EPSILON), in_specs=[v...  35 us
    pallas_call x1, Pallas kernels, q_project(): pl.pallas_call(q_kernel, grid=(steps,), in_specs=[pl.BlockSpec((rows, dep...  31.8 us
    pallas_call x1, Pallas kernels, value_heads(): pl.pallas_call(value_kernel, grid=(heads // (HEAD_PACK * GROUP),), in_spe...  13.7 us
    pallas_call x1, Pallas kernels, absorb(): pl.pallas_call(absorb_kernel, grid=(heads // (HEAD_PACK * GROUP),), in_sp...  13.3 us
    dot_general x1, matrix products, attention_rows(): jnp.dot(normed, w_dq, preferred_element_type=jnp.float32)  8.46 us
    dot_general x1, matrix products, attention_rows(): jnp.einsum('bhl,btl->bht', q_abs, ckv_cache, preferred_element_type=jnp.f...  6.36 us

profile of v3, /device:TPU:21, one launch (start us, length us, event | category | flops | bytes accessed | tf_op | source)
XLA Modules:
  0.0 236.3 jit_solution(4709143449975975327)
XLA Ops:
  0.7 1.2 fusion.4
  2.0 0.7 iota_compare_fusion
  2.7 0.8 copy.26
  3.5 0.8 copy.28
  4.3 0.1 copy.29
  4.4 4.6 %fusion.8 = f32[32,576]{1,0:T(8,128)S(1)} fusion(bf16[5120,576]{0,1:T(8,128)(2,1)} %param.29, bf16[32,5120]{1,0:T(8,128)(2,1)} %x_ref.1, f32[5120]{0:T(1024)} %param.25, f32[32]{0:T(128)S(1)} %add_rsqrt_fusion.2), kind=kOutput, calls=%fused_computation.17 | convolution fusion | flops 189399040 | bytes 6320256 | tf_op jit(solution)/shard_map/dot_general | solution.py:477
  9.1 0.1 multiply_reduce_fusion.1
  9.3 0.1 fusion.29
  9.4 0.7 pad_maximum_fusion.3
  10.1 0.7 fusion.19
  10.8 8.5 %multiply_reduce_fusion = (f32[32]{0:T(128)S(1)}, f32[32,1536]{1,0:T(8,128)S(1)}) fusion(bf16[5120,1536]{1,0:T(8,128)(2,1)} %param.26, bf16[32,5120]{1,0:T(8,128)(2,1)S(1)} %copy-done.3, f32[5120]{0:T(1024)S(1)} %copy-done.7, f32[32]{0:T(128)S(1)} %add_rsqrt_fusion.2), kind=kOutput, calls=%fused_computation.16 | convolution fusion | flops 504070112 | bytes 16273664 | tf_op jit(solution)/shard_map/dot_general | solution.py:475
  19.3 0.1 multiply_convert_fusion
  19.4 1.0 reshape.91.cos_ref
  20.4 1.0 reshape.92.sin_ref
  21.3 0.9 broadcast_bitcast_fusion.cq_ref
  22.3 31.8 %q_project.1 = (bf16[32,96,128]{2,1,0:T(8,128)(2,1)}, bf16[32,96,128]{2,1,0:T(8,128)(2,1)}) custom-call(bf16[256,1536]{1,0:T(8,128)(2,1)} %broadcast_bitcast_fusion.cq_ref, f32[4,256,1]{2,1,0:T(8,128)} %reshape.91.cos_ref, f32[4,256,1]{2,1,0:T(8,128)} %reshape.92.sin_ref, bf16[1536,192,128]{2,1,0:T(8,128)(2,1)} %bitcast.5.wa_ref.wb_ref, ...), custom_call_target="tpu_custom_call" | custom-call | flops 2415919104 | bytes 75497472 | tf_op jit(solution)/shard_map/q_project/pallas_call | solution.py:93
  54.1 1.0 slice.26
  55.0 1.1 slice.27
  56.1 0.9 fusion.7
  57.0 1.6 copy.33
  58.6 1.6 copy.32
  60.2 1.6 maximum_bitcast_fusion.q_ref
  61.7 13.3 %absorb.1 = bf16[32,128,512]{2,1,0:T(8,128)(2,1)} custom-call(bf16[32,128,128]{2,1,0:T(8,128)(2,1)} %maximum_bitcast_fusion.q_ref, bf16[512,128,128]{2,1,0:T(8,128)(2,1)} %w_ref.2), custom_call_target="tpu_custom_call" | custom-call | flops 536870912 | bytes 16777216 | tf_op jit(solution)/shard_map/absorb/pallas_call | solution.py:134
  75.0 4.1 %fusion.12 = f32[32,1,128]{2,1,0:T(1,128)} fusion(bf16[32,128,512]{2,1,0:T(8,128)(2,1)} %absorb.1, bf16[32,512,1]{1,0,2:T(8,128)(2,1)S(1)} %bitcast.35), kind=kOutput, calls=%fused_computation.19 | convolution fusion | flops 4194304 | bytes 4243456 | tf_op jit(solution)/shard_map/bhl,bl->bh/dot_general | solution.py:485
  79.2 6.4 %fusion.21 = f32[32,128,256]{2,1,0:T(8,128)S(1)} fusion(bf16[32,128,512]{2,1,0:T(8,128)(2,1)S(1)} %copy-done.2, bf16[32,256,512]{2,1,0:T(8,128)(2,1)} %param.20), kind=kOutput, calls=%fused_computation.40 | convolution fusion | flops 1073741824 | bytes 16777216 | tf_op jit(solution)/shard_map/bhl,btl->bht/dot_general | solution.py:481
  85.6 2.4 %fusion.20 = (f32[32,128]{1,0:T(8,128)S(1)}, f32[32,128,256]{2,1,0:T(8,128)S(1)}) fusion(f32[32,128,256]{2,1,0:T(8,128)S(1)} %fusion.21, bf16[32,256,64]{1,2,0:T(8,128)(2,1)S(1)} %copy-done, bf16[32,32,128]{2,1,0:T(8,128)(2,1)} %copy-done.5, bf16[32,32,128]{2,1,0:T(8,128)(2,1)} %copy-done.4, pred[32,256]{1,0:T(8,128)(4,1)S(1)} %iota_compare_fusion), kind=kOutput, calls=%fused_computation.39 | convolution fusion | flops 139456512 | bytes 9986048 | tf_op jit(solution)/shard_map/bhr,btr->bht/dot_general | solution.py:482
  88.0 1.3 fusion
  89.4 4.3 %divide_convert_fusion.l_ref = bf16[32,128,512]{2,1,0:T(8,128)(2,1)} fusion(f32[32,128]{1,0:T(8,128)S(1)} %get-tuple-element.16, f32[32,512]{1,0:T(8,128)S(1)} %copy-done.11, f32[32,128]{1,0:T(8,128)S(1)} %get-tuple-element.15, bf16[32,256,512]{2,1,0:T(8,128)(2,1)S(1)} %bitcast.31, f32[32,128,256]{2,1,0:T(8,128)S(1)} %get-tuple-element.20, ...), kind=kOutput, calls=%fused_computation | convolution fusion | flops 1084227584 | bytes 16891904 | tf_op jit(solution)/shard_map/bht,btl->bhl/dot_general | solution.py:491
  93.7 13.7 %value_heads.1.o_ref = bf16[32,16384]{1,0:T(8,128)(2,1)} custom-call(bf16[32,128,512]{2,1,0:T(8,128)(2,1)} %divide_convert_fusion.l_ref, bf16[512,128,128]{2,1,0:T(8,128)(2,1)} %w_ref.3), custom_call_target="tpu_custom_call" | custom-call | flops 536870912 | bytes 16777216 | tf_op jit(solution)/shard_map/value_heads/pallas_call | solution.py:171
  107.4 35.0 %pair_out.1 = (bf16[32,5120]{1,0:T(8,128)(2,1)}, bf16[32,5120]{1,0:T(8,128)(2,1)}) custom-call(bf16[32,16384]{1,0:T(8,128)(2,1)} %value_heads.1.o_ref, bf16[32,5120]{1,0:T(8,128)(2,1)} %x_ref.1, f32[1,5120]{1,0:T(1,128)} %bitcast.42, bf16[16384,5120]{1,0:T(8,128)(2,1)} %bitcast.14.w_hbm), custom_call_target="tpu_custom_call" | custom-call | tf_op jit(solution)/shard_map/pair_out/pallas_call | solution.py:458
  142.4 92.1 %mlp_group.1 = bf16[32,5120]{1,0:T(8,128)(2,1)} custom-call(bf16[2,16,5120]{2,1,0:T(8,128)(2,1)} %bitcast.34, bf16[32,5120]{1,0:T(8,128)(2,1)} %get-tuple-element.10.r_ref, bf16[5120,768]{1,0:T(8,128)(2,1)} %gate_hbm.1, bf16[5120,768]{1,0:T(8,128)(2,1)} %up_hbm.1, bf16[768,5120]{1,0:T(8,128)(2,1)} %down_hbm.1), custom_call_target="tpu_custom_call" | custom-call | tf_op jit(solution)/shard_map/mlp_group/pallas_call | solution.py:372
  234.6 1.7 copy.43
  (42 shorter events, 0.3 us)
Async XLA Ops:
  0.6 84.9 %copy-start = (bf16[32,256,64]{1,2,0:T(8,128)(2,1)S(1)}, bf16[32,256,64]{1,2,0:T(8,128)(2,1)}, u32[]{:S(2)}) copy-start(bf16[32,256,64]{1,2,0:T(8,128)(2,1)} %param.21) | copy-start | bytes 3145732
  0.6 10.1 %copy-start.3 = (bf16[32,5120]{1,0:T(8,128)(2,1)S(1)}, bf16[32,5120]{1,0:T(8,128)(2,1)}, u32[]{:S(2)}) copy-start(bf16[32,5120]{1,0:T(8,128)(2,1)} %x_ref.1) | copy-start | bytes 983044
  0.7 10.1 %copy-start.7 = (f32[5120]{0:T(1024)S(1)}, f32[5120]{0:T(1024)}, u32[]{:S(2)}) copy-start(f32[5120]{0:T(1024)} %param.25) | copy-start | bytes 61444
  0.7 8.5 %copy-start.10 = (f32[32,32]{1,0:T(8,128)S(1)}, f32[32,32]{1,0:T(8,128)}, u32[]{:S(2)}) copy-start(f32[32,32]{1,0:T(8,128)} %param.24) | copy-start | bytes 12292
  0.7 8.5 %copy-start.9 = (f32[32,32]{1,0:T(8,128)S(1)}, f32[32,32]{1,0:T(8,128)}, u32[]{:S(2)}) copy-start(f32[32,32]{1,0:T(8,128)} %param.23) | copy-start | bytes 12292
  0.7 9.4 %copy-start.14 = (f32[512]{0:T(512)S(1)}, f32[512]{0:T(512)}, u32[]{:S(2)}) copy-start(f32[512]{0:T(512)} %param.30) | copy-start | bytes 6148
  10.8 64.3 %copy-start.6 = (bf16[32,512]{1,0:T(8,128)(2,1)}, bf16[32,512]{1,0:T(8,128)(2,1)S(1)}, u32[]{:S(2)}) copy-start(bf16[32,512]{1,0:T(8,128)(2,1)S(1)} %get-tuple-element.25) | copy-start | bytes 98308
  10.8 8.5 %copy-start.13 = (f32[1536]{0:T(1024)S(1)}, f32[1536]{0:T(1024)}, u32[]{:S(2)}) copy-start(f32[1536]{0:T(1024)} %param.27) | copy-start | bytes 18436
  55.0 1.9 copy-start.4
  56.1 0.9 copy-start.5
  75.0 4.1 %copy-start.2 = (bf16[32,128,512]{2,1,0:T(8,128)(2,1)S(1)}, bf16[32,128,512]{2,1,0:T(8,128)(2,1)}, u32[]{:S(2)}) copy-start(bf16[32,128,512]{2,1,0:T(8,128)(2,1)} %absorb.1) | copy-start | bytes 12582916
  79.2 10.2 %slice-start = ((s8[8388608]{0:T(1024)(128)(4,1)}), s8[4194304]{0:T(1024)(128)(4,1)S(1)}, s32[]{:S(2)}) async-start(s8[8388608]{0:T(1024)(128)(4,1)} %bitcast.30), calls=%async_computation | async-start | bytes 8388608
  79.2 10.2 %slice-start.1 = ((s8[8388608]{0:T(1024)(128)(4,1)}), s8[4194304]{0:T(1024)(128)(4,1)S(1)}, s32[]{:S(2)}) async-start(s8[8388608]{0:T(1024)(128)(4,1)} %bitcast.30), calls=%async_computation.1 | async-start | bytes 8388608
  85.6 2.4 %copy-start.8 = (f32[32,1,128]{2,1,0:T(1,128)S(1)}, f32[32,1,128]{2,1,0:T(1,128)}, u32[]{:S(2)}) copy-start(f32[32,1,128]{2,1,0:T(1,128)} %fusion.12) | copy-start | bytes 49156
  85.6 2.4 %copy-start.12 = (f32[32,1,128]{2,1,0:T(1,128)S(1)}, f32[32,1,128]{2,1,0:T(1,128)}, u32[]{:S(2)}) copy-start(f32[32,1,128]{2,1,0:T(1,128)} %fusion.7) | copy-start | bytes 49156
  88.0 1.4 copy-start.11
  142.4 93.9 %copy-start.1 = (bf16[32,256,64]{1,2,0:T(8,128)(2,1)S(1)}, bf16[32,256,64]{1,2,0:T(8,128)(2,1)}, u32[]{:S(2)}) copy-start(bf16[32,256,64]{1,2,0:T(8,128)(2,1)} %param.21) | copy-start | bytes 3145732

commit v4 on v3

--- a/solution.py
+++ b/solution.py
@@ -68,12 +68,11 @@
         ob_ref[:, part * GROUP:(part + 1) * GROUP, :] = second.reshape(batch, GROUP, LANES).astype(jnp.bfloat16)
 
 
-def q_project(q_latent, w_uq, rope_cos, rope_sin):
-    batch, depth = q_latent.shape
+def q_project(repeated, w_uq, rope_cos, rope_sin):
+    batch, depth = rope_cos.shape[0], repeated.shape[1]
     heads, width = w_uq.shape[1], w_uq.shape[2]
     stored = jnp.transpose(w_uq, (0, 2, 1))
     rows = batch * GROUP
-    repeated = jnp.broadcast_to(q_latent[:, None, :], (batch, GROUP, depth)).reshape(rows, depth)
     half = rope_cos.shape[1]
     turns = half // (GROUP * Q_PACK)
     nope = (width - 2 * half) // (2 * GROUP * Q_PACK)
@@ -103,21 +102,31 @@
         cost_estimate=pl.CostEstimate(flops=2 * batch * depth * heads * width, bytes_accessed=2 * depth * heads * width, transcendentals=0),
         name='q_project',
     )(repeated, cos_c, sin_c, stored, stored)
-    cut = nope * Q_PACK * GROUP
-    q_nope = jnp.concatenate([out_a[:, :cut], out_b[:, :cut]], axis=1).transpose(0, 2, 1)
-    q_pe = jnp.concatenate([out_a[:, cut:], out_b[:, cut:]], axis=1).transpose(0, 2, 1)
-    return q_nope, q_pe
-
-
-def absorb_kernel(q_ref, w_ref, o_ref, plain):
-    batch, heads, inner = q_ref.shape
-    outer = w_ref.shape[0]
+    return out_a, out_b
+
+
+def absorb_kernel(a_ref, b_ref, w_ref, o_ref, plain, turned):
+    batch, half, heads = a_ref.shape
+    packed = turned.shape[2]
+    outer, inner = w_ref.shape[0], w_ref.shape[2]
     rows = batch * GROUP
     own = lane_ids((rows, inner), 0) % GROUP
-    for part in range(heads // GROUP):
+    step = pl.program_id(0)
+
+    @pl.when(step == 0)
+    def _():
+        def turn(row, carry):
+            flat = jnp.concatenate([a_ref[row], b_ref[row]], axis=0).astype(jnp.float32).T.astype(jnp.bfloat16)
+            for part in range(heads // packed):
+                turned[part, row] = flat[part * packed:(part + 1) * packed, :]
+            return carry
+
+        lax.fori_loop(0, batch, turn, 0)
+
+    for part in range(packed // GROUP):
         span = slice(part * GROUP, (part + 1) * GROUP)
         plain[part] = w_ref[:, span, :].reshape(outer * GROUP, inner).astype(jnp.float32)
-        queries = q_ref[:, span, :].reshape(rows, inner)
+        queries = turned[step, :, span, :].reshape(rows, inner)
         acc = jnp.zeros((rows, outer), jnp.float32)
         for h in range(0, GROUP, 2):
             left = jnp.concatenate([jnp.where(own == h, queries, jnp.zeros_like(queries)),
@@ -128,21 +137,124 @@
         o_ref[:, span, :] = acc.reshape(batch, GROUP, outer).astype(jnp.bfloat16)
 
 
-def absorb(q_nope, w_uk):
-    batch, heads, inner = q_nope.shape
-    outer = w_uk.shape[0]
+def absorb(out_a, out_b, w_uk):
+    batch, heads = out_a.shape[0], out_a.shape[2]
+    outer, inner = w_uk.shape[0], w_uk.shape[2]
+    packed = HEAD_PACK * GROUP
+    half_spec = pl.BlockSpec((batch, inner // 2, heads), lambda g: (0, 0, 0))
     return pl.pallas_call(
         absorb_kernel,
-        grid=(heads // (HEAD_PACK * GROUP),),
-        in_specs=[pl.BlockSpec((batch, HEAD_PACK * GROUP, inner), lambda g: (0, g, 0)),
-                  pl.BlockSpec((outer, HEAD_PACK * GROUP, inner), lambda g: (0, g, 0))],
-        out_specs=pl.BlockSpec((batch, HEAD_PACK * GROUP, outer), lambda g: (0, g, 0)),
+        grid=(heads // packed,),
+        in_specs=[half_spec, half_spec, pl.BlockSpec((outer, packed, inner), lambda g: (0, g, 0))],
+        out_specs=pl.BlockSpec((batch, packed, outer), lambda g: (0, g, 0)),
         out_shape=jax.ShapeDtypeStruct((batch, heads, outer), jnp.bfloat16),
-        scratch_shapes=[pltpu.VMEM((HEAD_PACK, outer * GROUP, inner), jnp.float32)],
+        scratch_shapes=[pltpu.VMEM((HEAD_PACK, outer * GROUP, inner), jnp.float32), pltpu.VMEM((heads // packed, batch, packed, inner), jnp.bfloat16)],
         compiler_params=pltpu.CompilerParams(vmem_limit_bytes=VMEM_BYTES),
         cost_estimate=pl.CostEstimate(flops=2 * batch * heads * inner * outer, bytes_accessed=2 * heads * inner * outer, transcendentals=0),
         name='absorb',
-    )(q_nope, w_uk)
+    )(out_a, out_b, w_uk)
+
+
+REQUESTS = 8
+TOGETHER = 4
+
+
+def attend_kernel(scale, len_ref, q_ref, ra_ref, rb_ref, ckv_ref, kpe_ref, c_ref, k_ref, o_ref):
+    count = q_ref.shape[0]
+    base = pl.program_id(0) * count
+    for start in range(0, count, TOGETHER):
+        group = range(start, start + TOGETHER)
+        rotary = {i: jnp.concatenate([ra_ref[i], rb_ref[i]], axis=0).astype(jnp.float32).T for i in group}
+        scores = {i: (lax.dot_general(q_ref[i], ckv_ref[i], (((1,), (1,)), ((), ())), preferred_element_type=jnp.float32)
+                      + jnp.dot(rotary[i].astype(jnp.bfloat16), kpe_ref[i], preferred_element_type=jnp.float32)) * scale for i in group}
+        fresh = {i: c_ref[i:i + 1, :] for i in group}
+        score_new = {i: (jnp.sum(q_ref[i].astype(jnp.float32) * fresh[i], axis=-1, keepdims=True)
+                         + jnp.sum(rotary[i] * k_ref[i:i + 1, :], axis=-1, keepdims=True)) * scale for i in group}
+        scores = {i: jnp.where(lane_ids(scores[i].shape, 1) < len_ref[base + i], scores[i], -jnp.inf) for i in group}
+        row_max = {i: jnp.maximum(jnp.max(scores[i], axis=-1, keepdims=True), score_new[i]) for i in group}
+        exp_cache = {i: jnp.exp(scores[i] - row_max[i]) for i in group}
+        exp_new = {i: jnp.exp(score_new[i] - row_max[i]) for i in group}
+        weighted = {i: jnp.dot(exp_cache[i].astype(jnp.bfloat16), ckv_ref[i], preferred_element_type=jnp.float32) for i in group}
+        norm_sum = {i: jnp.sum(exp_cache[i], axis=-1, keepdims=True) + exp_new[i] for i in group}
+        for i in group:
+            total = weighted[i] + exp_new[i].astype(jnp.bfloat16).astype(jnp.float32) * fresh[i]
+            o_ref[i] = (total / norm_sum[i]).astype(jnp.bfloat16)
+
+
+def attend(scale, q_abs, out_a, out_b, ckv_cache, kpe_cache, cache_len, ckv_new, kpe_new):
+    batch, heads, outer = q_abs.shape
+    past, rotary = kpe_cache.shape[1], kpe_cache.shape[2]
+    half = rotary // 2
+    last = out_a.shape[1] // half - 1
+    turn_spec = pl.BlockSpec((REQUESTS, half, heads), lambda b: (b, last, 0))
+    return pl.pallas_call(
+        functools.partial(attend_kernel, scale),
+        grid=(batch // REQUESTS,),
+        in_specs=[pl.BlockSpec(memory_space=pltpu.SMEM), pl.BlockSpec((REQUESTS, heads, outer), lambda b: (b, 0, 0)), turn_spec, turn_spec,
+                  pl.BlockSpec((REQUESTS, past, outer), lambda b: (b, 0, 0)), pl.BlockSpec((REQUESTS, rotary, past), lambda b: (b, 0, 0)),
+                  pl.BlockSpec((REQUESTS, outer), lambda b: (b, 0)), pl.BlockSpec((REQUESTS, rotary), lambda b: (b, 0))],
+        out_specs=pl.BlockSpec((REQUESTS, heads, outer), lambda b: (b, 0, 0)),
+        out_shape=jax.ShapeDtypeStruct((batch, heads, outer), jnp.bfloat16),
+        compiler_params=pltpu.CompilerParams(vmem_limit_bytes=VMEM_BYTES),
+        cost_estimate=pl.CostEstimate(flops=4 * batch * heads * past * outer, bytes_accessed=2 * batch * past * outer, transcendentals=0),
+        name='attend',
+    )(cache_len, q_abs, out_a, out_b, ckv_cache, kpe_cache.transpose(0, 2, 1), ckv_new, kpe_new)
+
+
+FRONT_DEPTH = 1024
+
+
+def front_kernel(x_ref, g_ref, wq_ref, wkv_ref, gq_ref, gkv_ref, cos_ref, sin_ref, q_ref, c_ref, k_ref, c_wide, k_wide, normed, q_acc, kv_acc):
+    step = pl.program_id(0)
+    depth = wq_ref.shape[0]
+
+    @pl.when(step == 0)
+    def _():
+        normed[...] = rms_norm(x_ref[...], g_ref[...]).astype(jnp.bfloat16)
+        q_acc[...] = jnp.zeros_like(q_acc)
+        kv_acc[...] = jnp.zeros_like(kv_acc)
+
+    part = normed[:, pl.ds(pl.multiple_of(step * depth, depth), depth)]
+    q_acc[...] += jnp.dot(part, wq_ref[...], preferred_element_type=jnp.float32)
+    kv_acc[...] += lax.dot_general(part, wkv_ref[...], (((1,), (1,)), ((), ())), preferred_element_type=jnp.float32)
+
+    @pl.when(step == pl.num_programs(0) - 1)
+    def _():
+        q_latent = rms_norm(q_acc[...], gq_ref[...]).astype(jnp.bfloat16)
+        rows = (q_ref.shape[0], q_latent.shape[0])
+        repeat = (lane_ids(rows, 0) // GROUP == lane_ids(rows, 1)).astype(jnp.bfloat16)
+        q_ref[...] = jnp.dot(repeat, q_latent, preferred_element_type=jnp.float32).astype(jnp.bfloat16)
+        inner = c_ref.shape[1]
+        kv = kv_acc[...]
+        c_new = rms_norm(kv[:, :inner], gkv_ref[...]).astype(jnp.bfloat16)
+        k_new = apply_rope(kv[:, inner:], cos_ref[...], sin_ref[...]).astype(jnp.bfloat16)
+        c_ref[...] = c_new
+        k_ref[...] = k_new
+        c_wide[...] = c_new.astype(jnp.float32)
+        k_wide[...] = k_new.astype(jnp.float32)
+
+
+def front(hidden, rope_cos, rope_sin, norm_attn, w_dq, norm_q, w_dkv, norm_kv):
+    batch, width = hidden.shape
+    latent = w_dq.shape[1]
+    joint = w_dkv.shape[1]
+    inner = norm_kv.shape[0]
+
+    def whole(*shape):
+        return pl.BlockSpec(shape, lambda k: (0,) * len(shape))
+
+    half = rope_cos.shape[1]
+    return pl.pallas_call(
+        front_kernel,
+        grid=(width // FRONT_DEPTH,),
+        in_specs=[whole(batch, width), whole(1, width), pl.BlockSpec((FRONT_DEPTH, latent), lambda k: (k, 0)), pl.BlockSpec((joint, FRONT_DEPTH), lambda k: (0, k)),
+                  whole(1, latent), whole(1, inner), whole(batch, half), whole(batch, half)],
+        out_specs=[whole(batch * GROUP, latent)] + [whole(batch, inner), whole(batch, joint - inner)] * 2,
+        out_shape=[jax.ShapeDtypeStruct((batch * GROUP, latent), jnp.bfloat16)] + [jax.ShapeDtypeStruct((batch, size), kind) for kind in (jnp.bfloat16, jnp.float32) for size in (inner, joint - inner)],
+        scratch_shapes=[pltpu.VMEM((batch, width), jnp.bfloat16), pltpu.VMEM((batch, latent), jnp.float32), pltpu.VMEM((batch, joint), jnp.float32)],
+        compiler_params=pltpu.CompilerParams(vmem_limit_bytes=VMEM_BYTES),
+        name='front',
+    )(hidden, norm_attn[None, :], w_dq, w_dkv.T, norm_q[None, :], norm_kv[None, :], rope_cos, rope_sin)
 
 
 def value_kernel(l_ref, w_ref, o_ref, plain, picked):
@@ -468,33 +580,13 @@
     )(head_out, hidden, norm_mlp[None, :], w_flat)
 
 
-def attention_rows(axis, hidden, ckv_cache, kpe_cache, cache_len, rope_cos, rope_sin, norm_attn, w_dq, norm_q, w_uq, w_dkv, norm_kv, w_uk, w_uv, w_out, norm_mlp):
-    value_a7 = w_uk.shape[0]
+def attention_heads(hidden, ckv_cache, kpe_cache, cache_len, rope_cos, rope_sin, norm_attn, w_dq, norm_q, w_uq, w_dkv, norm_kv, w_uk, w_uv):
     score_scale = MSCALE * MSCALE / math.sqrt(w_uq.shape[2])
-    normed = rms_norm(hidden, norm_attn).astype(jnp.bfloat16)
-    q_latent = rms_norm(jnp.dot(normed, w_dq, preferred_element_type=jnp.float32), norm_q).astype(jnp.bfloat16)
-    q_nope, q_pe = q_project(q_latent, w_uq, rope_cos, rope_sin)
-    kv_full = jnp.dot(normed, w_dkv, preferred_element_type=jnp.float32)
-    ckv_new = rms_norm(kv_full[:, :value_a7], norm_kv).astype(jnp.bfloat16)
-    kpe_new = apply_rope(kv_full[:, value_a7:], rope_cos, rope_sin).astype(jnp.bfloat16)
-    q_abs = absorb(q_nope, w_uk)
-    scores = (jnp.einsum('bhl,btl->bht', q_abs, ckv_cache, preferred_element_type=jnp.float32)
-              + jnp.einsum('bhr,btr->bht', q_pe, kpe_cache, preferred_element_type=jnp.float32)) * score_scale
-    positions = jnp.arange(ckv_cache.shape[1])
-    scores = jnp.where(positions[None, None, :] < cache_len[:, None, None], scores, -jnp.inf)
-    score_new = (jnp.einsum('bhl,bl->bh', q_abs, ckv_new, preferred_element_type=jnp.float32)
-                 + jnp.einsum('bhr,br->bh', q_pe, kpe_new, preferred_element_type=jnp.float32)) * score_scale
-    row_max = jnp.maximum(jnp.max(scores, axis=-1), score_new)
-    exp_cache = jnp.exp(scores - row_max[..., None])
-    exp_new = jnp.exp(score_new - row_max)
-    norm_sum = jnp.sum(exp_cache, axis=-1) + exp_new
-    weighted = (jnp.einsum('bht,btl->bhl', exp_cache.astype(jnp.bfloat16), ckv_cache, preferred_element_type=jnp.float32)
-                + exp_new.astype(jnp.bfloat16).astype(jnp.float32)[..., None] * ckv_new.astype(jnp.float32)[:, None, :])
-    lat_out = (weighted / norm_sum[..., None]).astype(jnp.bfloat16)
-    head_out = value_heads(lat_out, w_uv)
-    w_flat = w_out.reshape(w_out.shape[0] * w_out.shape[1], w_out.shape[2])
-    residual, mlp_in = pair_out(axis, head_out, hidden, w_flat, norm_mlp)
-    return residual, mlp_in, ckv_new, kpe_new
+    repeated, ckv_new, kpe_new, ckv_wide, kpe_wide = front(hidden, rope_cos, rope_sin, norm_attn, w_dq, norm_q, w_dkv, norm_kv)
+    out_a, out_b = q_project(repeated, w_uq, rope_cos, rope_sin)
+    q_abs = absorb(out_a, out_b, w_uk)
+    lat_out = attend(score_scale, q_abs, out_a, out_b, ckv_cache, kpe_cache, cache_len, ckv_wide, kpe_wide)
+    return value_heads(lat_out, w_uv), ckv_new, kpe_new
 
 
 def solution(mesh):
@@ -506,7 +598,9 @@
                 P(None, 'dp'), P(None, 'dp'), P('dp', None))
 
     def local_step(hidden, ckv_cache, kpe_cache, cache_len, rope_cos, rope_sin, norm_attn, w_dq, norm_q, w_uq, w_dkv, norm_kv, w_uk, w_uv, w_out, norm_mlp, w_gate, w_up, w_down):
-        residual, mlp_in, ckv_new, kpe_new = attention_rows('dp', hidden, ckv_cache, kpe_cache, cache_len, rope_cos, rope_sin, norm_attn, w_dq, norm_q, w_uq, w_dkv, norm_kv, w_uk, w_uv, w_out, norm_mlp)
+        head_out, ckv_new, kpe_new = attention_heads(hidden, ckv_cache, kpe_cache, cache_len, rope_cos, rope_sin, norm_attn, w_dq, norm_q, w_uq, w_dkv, norm_kv, w_uk, w_uv)
+        w_flat = w_out.reshape(w_out.shape[0] * w_out.shape[1], w_out.shape[2])
+        residual, mlp_in = pair_out('dp', head_out, hidden, w_flat, norm_mlp)
         out_hidden = mlp_group('dp', mesh.shape['dp'], mlp_in, residual, w_gate, w_up, w_down)
         return out_hidden, ckv_new, kpe_new
 

time: 237 us -> 220 us (0.928)
  matrix products: 31.1 us -> 0 us
  Pallas kernels: 186 us -> 212 us
  other arithmetic: 6.66 us -> 0 us
  local copies, waits for them, and re-layouts: 11.7 us -> 6.76 us
    dot_general x7 -> x0, matrix products: 31.1 us -> none  [the longest x1 8.46 us: attention_rows(): jnp.dot(normed, w_dq, preferred_element_type=jnp.float32)]
    pallas_call x1 -> x3, Pallas kernels: 13.3 us -> 38.9 us  [the longest x1 16.9 us: absorb(): pl.pallas_call(absorb_kernel, grid=(heads // packed,), in_specs=[half_spe...]
    pallas_call x2 -> x0, local copies, waits for them, and re-layouts: 3.15 us -> none  [q_project(): pl.pallas_call(q_kernel, grid=(steps,), in_specs=[pl.BlockSpec((rows, dep...]
    reduce_sum x3 -> x0, other arithmetic: 2.7 us -> none  [the longest x2 1.37 us: rms_norm(): mean_sq = jnp.mean(floats * floats, axis=-1, keepdims=True)]
where the time goes in v4:
time: 220 us; the launch traced here: 219 us
  Pallas kernels  212 us (96%)
  local copies, waits for them, and re-layouts  6.76 us (3%)
    pallas_call x1, Pallas kernels, mlp_group(): pl.pallas_call(functools.partial(mlp_kernel, axis, chips), in_specs=[vmem...  92.1 us
    pallas_call x1, Pallas kernels, pair_out(): pl.pallas_call(functools.partial(pair_kernel, axis, EPSILON), in_specs=[v...  35.2 us
    pallas_call x1, Pallas kernels, q_project(): pl.pallas_call(q_kernel, grid=(steps,), in_specs=[pl.BlockSpec((rows, dep...  31.8 us
    pallas_call x1, Pallas kernels, absorb(): pl.pallas_call(absorb_kernel, grid=(heads // packed,), in_specs=[half_spe...  16.9 us
    pallas_call x1, Pallas kernels, value_heads(): pl.pallas_call(value_kernel, grid=(heads // (HEAD_PACK * GROUP),), in_spe...  13.7 us
    pallas_call x1, Pallas kernels, front(): pl.pallas_call(front_kernel, grid=(width // FRONT_DEPTH,), in_specs=[whol...  11.4 us
    pallas_call x1, Pallas kernels, attend(): pl.pallas_call(functools.partial(attend_kernel, scale), grid=(batch // RE...  10.5 us

profile of v4, /device:TPU:21, one launch (start us, length us, event | category | flops | bytes accessed | tf_op | source)
XLA Modules:
  0.0 219.1 jit_solution(3829178438449068401)
XLA Ops:
  0.6 1.3 broadcast_in_dim.13.gq_ref
  1.9 0.8 copy.24
  2.7 0.8 copy.26
  3.5 0.1 copy.27
  3.6 0.1 copy.25
  3.7 1.0 reshape.30.cos_ref
  4.7 1.0 reshape.31.sin_ref
  5.7 11.4 %front.1 = (bf16[256,1536]{1,0:T(8,128)(2,1)}, bf16[32,512]{1,0:T(8,128)(2,1)}, bf16[32,64]{1,0:T(8,128)(2,1)}, f32[32,512]{1,0:T(8,128)}, f32[32,64]{1,0:T(8,128)}) custom-call(bf16[32,5120]{1,0:T(8,128)(2,1)} %x_ref.3, f32[1,5120]{1,0:T(1,128)} %bitcast.19, bf16[5120,1536]{1,0:T(8,128)(2,1)} %wq_ref.1, bf16[576,5120]{1,0:T(8,128)(2,1)} %bitcast.14, ...), custom_call_target="tpu_custom_call" | custom-call | tf_op jit(solution)/shard_map/front/pallas_call | solution.py:247
  17.1 31.8 %q_project.1 = (bf16[32,96,128]{2,1,0:T(8,128)(2,1)}, bf16[32,96,128]{2,1,0:T(8,128)(2,1)}) custom-call(bf16[256,1536]{1,0:T(8,128)(2,1)} %get-tuple-element.12.cq_ref, f32[4,256,1]{2,1,0:T(8,128)} %reshape.30.cos_ref, f32[4,256,1]{2,1,0:T(8,128)} %reshape.31.sin_ref, bf16[1536,192,128]{2,1,0:T(8,128)(2,1)} %bitcast.7.wa_ref.wb_ref, ...), custom_call_target="tpu_custom_call" | custom-call | flops 2415919104 | bytes 75497472 | tf_op jit(solution)/shard_map/q_project/pallas_call | solution.py:92
  48.9 16.9 %absorb.1.q_ref = bf16[32,128,512]{2,1,0:T(8,128)(2,1)} custom-call(bf16[32,96,128]{2,1,0:T(8,128)(2,1)} %get-tuple-element.13.a_ref.ra_ref, bf16[32,96,128]{2,1,0:T(8,128)(2,1)} %get-tuple-element.14.b_ref.rb_ref, bf16[512,128,128]{2,1,0:T(8,128)(2,1)} %w_ref.2), custom_call_target="tpu_custom_call" | custom-call | flops 536870912 | bytes 16777216 | tf_op jit(solution)/shard_map/absorb/pallas_call | solution.py:145
  65.9 10.5 %attend.1.l_ref = bf16[32,128,512]{2,1,0:T(8,128)(2,1)} custom-call(s32[32]{0:T(128)} %len_ref.1, bf16[32,128,512]{2,1,0:T(8,128)(2,1)} %absorb.1.q_ref, bf16[32,96,128]{2,1,0:T(8,128)(2,1)} %get-tuple-element.13.a_ref.ra_ref, bf16[32,96,128]{2,1,0:T(8,128)(2,1)} %get-tuple-element.14.b_ref.rb_ref, bf16[32,256,512]{2,1,0:T(8,128)(2,1)} %ckv_ref.1, ...), custom_call_target="tpu_custom_call" | custom-call | flops 2147483648 | bytes 8388608 | tf_op jit(solution)/shard_map/attend/pallas_call | solution.py:190
  76.4 13.7 %value_heads.1.o_ref = bf16[32,16384]{1,0:T(8,128)(2,1)} custom-call(bf16[32,128,512]{2,1,0:T(8,128)(2,1)} %attend.1.l_ref, bf16[512,128,128]{2,1,0:T(8,128)(2,1)} %w_ref.3), custom_call_target="tpu_custom_call" | custom-call | flops 536870912 | bytes 16777216 | tf_op jit(solution)/shard_map/value_heads/pallas_call | solution.py:283
  90.1 35.2 %pair_out.1 = (bf16[32,5120]{1,0:T(8,128)(2,1)}, bf16[32,5120]{1,0:T(8,128)(2,1)}) custom-call(bf16[32,16384]{1,0:T(8,128)(2,1)} %value_heads.1.o_ref, bf16[32,5120]{1,0:T(8,128)(2,1)} %x_ref.3, f32[1,5120]{1,0:T(1,128)} %bitcast.20, bf16[16384,5120]{1,0:T(8,128)(2,1)} %bitcast.10.w_hbm), custom_call_target="tpu_custom_call" | custom-call | tf_op jit(solution)/shard_map/pair_out/pallas_call | solution.py:570
  125.3 92.1 %mlp_group.1 = bf16[32,5120]{1,0:T(8,128)(2,1)} custom-call(bf16[2,16,5120]{2,1,0:T(8,128)(2,1)} %bitcast.16, bf16[32,5120]{1,0:T(8,128)(2,1)} %get-tuple-element.18.r_ref, bf16[5120,768]{1,0:T(8,128)(2,1)} %gate_hbm.1, bf16[5120,768]{1,0:T(8,128)(2,1)} %up_hbm.1, bf16[768,5120]{1,0:T(8,128)(2,1)} %down_hbm.1), custom_call_target="tpu_custom_call" | custom-call | tf_op jit(solution)/shard_map/mlp_group/pallas_call | solution.py:484
  217.4 1.7 copy.31
